TPU v7x, 256 devices: a whole 4x4x8 slice. The times are simulated.
256 devices in a mesh: gx: 32 (over x, z), gy: 8 (over y, core).
Axes of the slice: x: 4, y: 4, z: 8, core: 2. Of those that a mesh axis runs over, the one named last changes fastest.
Arguments:
- dense_grads: float32 [256, 2048, 1024], P(('gx', 'gy')), may hold values from -24 to 24
- dense_param: float32 [2048, 1024], P(('gx', 'gy')), may hold values from -6 to 6
- dense_acc: float32 [2048, 1024], P(('gx', 'gy'))
- table: float32 [1048576, 128], P(('gx', 'gy')), may hold values from -6 to 6
- row_acc: float32 [1048576], P(('gx', 'gy'))
- touched: int32 [131072], P(('gx', 'gy')), may hold values from 0 to 4095, as said below
- emb_grads: float32 [131072, 128], P(('gx', 'gy'))
Outputs:
- new_dense: float32 [2048, 1024], P(('gx', 'gy'))
- new_dense_acc: float32 [2048, 1024], P(('gx', 'gy'))
- new_table: float32 [1048576, 128], P(('gx', 'gy'))
- new_row_acc: float32 [1048576], P(('gx', 'gy'))
Inputs may be any that keep to these rules, and one draw needn't show every extreme that they name: `touched`: within one device's 512 entries no row number repeats.
All inputs are finite; a program needn't handle non-finite values.
Results may differ from a plain program's by a relative error of at most 0.000022.
Values sent between devices are 32-bit elements; how exact they have to be, the bound alone decides.
A program may use at most 128 MiB of HBM per device.

v0:
```python
import jax
import jax.numpy as jnp
from jax import lax
from jax.sharding import PartitionSpec as P

learn_rate = 0.5
max_norm = 8.0
epsilon = 1e-10


def body(dense_grads, dense_param, dense_acc, table, row_acc, touched, emb_grads):
    shards = lax.axis_size(("gx", "gy"))
    local_grad = dense_grads[0]
    embed_square = jnp.sum(emb_grads * emb_grads)
    own_rows = dense_param.shape[0]
    summed, embed_total = lax.psum((local_grad, embed_square), ("gx", "gy"))
    mean_whole = summed / jnp.float32(shards)
    norm_sq = jnp.sum(mean_whole * mean_whole) + embed_total
    start = lax.axis_index(("gx", "gy")) * own_rows
    mean_grad = lax.dynamic_slice_in_dim(mean_whole, start, own_rows, 0)
    clip = jnp.minimum(jnp.float32(1.0), max_norm / (jnp.sqrt(norm_sq) + 1e-06))
    scaled = clip * mean_grad
    new_dense_acc = dense_acc + scaled * scaled
    new_dense = dense_param - learn_rate * scaled / (jnp.sqrt(new_dense_acc) + epsilon)
    row_grads = clip * emb_grads
    square_mean = jnp.mean(row_grads * row_grads, axis=1)
    updated_acc = row_acc[touched] + square_mean
    new_row_acc = row_acc.at[touched].set(updated_acc)
    updated_rows = (
        table[touched] - learn_rate * row_grads / (jnp.sqrt(updated_acc) + epsilon)[:, None]
    )
    new_table = table.at[touched].set(updated_rows)
    return (new_dense, new_dense_acc, new_table, new_row_acc)


def solution(mesh):
    return jax.shard_map(
        body,
        mesh=mesh,
        in_specs=(
            P(("gx", "gy"), None, None),
            P(("gx", "gy"), None),
            P(("gx", "gy"), None),
            P(("gx", "gy"), None),
            P(("gx", "gy")),
            P(("gx", "gy")),
            P(("gx", "gy"), None),
        ),
        out_specs=(
            P(("gx", "gy"), None),
            P(("gx", "gy"), None),
            P(("gx", "gy"), None),
            P(("gx", "gy")),
        ),
        check_vma=False,
    )
```

profile of v0, /device:TPU:1, one launch (start us, length us, event | category | flops | bytes accessed | tf_op | source)
XLA Modules:
  0.0 320.8 jit_solution(18132003052259875180)
XLA Ops:
  7.2 0.0 copy-start.6
  7.2 0.0 all-reduce.2.cloned.1.call-start
  7.2 0.7 copy-done.6
  7.9 0.0 all-reduce.2.cloned.1.call-update
  7.9 0.9 copy-done.3
  8.8 0.7 multiply_reduce_fusion.2
  9.5 81.4 %psum.15 = f32[]{:T(128)} all-reduce(f32[]{:T(128)} %multiply_reduce_fusion.2), channel_id=1, replica_groups=mesh['gx'=32,'gy'=8] {'gx','gy'}, use_global_device_ids=true, to_apply=%region_3.0 | all-reduce | flops 1 | bytes 8 | tf_op jit(solution)/shard_map/psum | solution.py:16
  90.9 0.0 copy-done.7
  90.9 3.1 gather_fusion
  94.1 201.4 %all-reduce.2.cloned.1.call-done = f32[2048,1024]{1,0:T(8,128)} async-done(((f32[2048,1024]{1,0:T(8,128)}), f32[2048,1024]{1,0:T(8,128)}) %all-reduce.2.cloned.1.call-update) | async-done | bytes 8388624 | tf_op jit(solution)/shard_map/psum | solution.py:16
  295.4 9.4 %multiply_reduce_fusion = (f32[]{:T(128)}, f32[2048,1024]{1,0:T(8,128)}) fusion(f32[2048,1024]{1,0:T(8,128)} %all-reduce.2.cloned.1.call-done), kind=kLoop, calls=%fused_computation.4 | loop fusion | flops 6291455 | bytes 16777220 | tf_op jit(solution)/shard_map/reduce_sum | solution.py:18
  306.2 0.1 multiply_reduce_fusion.1
  306.4 0.0 copy-start.2
  306.4 2.5 scatter_fusion
  308.9 0.0 copy-start
  308.9 0.0 copy-done.2
  308.9 0.0 copy-start.4
  308.9 0.0 copy-start.5
  308.9 3.6 %scatter_custom_fusion = f32[4096,128]{1,0:T(8,128)S(1)} fusion(f32[4096,128]{1,0:T(8,128)S(1)} %copy-done.2, s32[512]{0:T(512)S(1)} %compare_select_fusion, f32[512,128]{1,0:T(8,128)S(1)} %copy-done.3, f32[512]{0:T(512)S(1)} %get-tuple-element.4, f32[]{:T(128)} %constant.13.clone.1, f32[]{:T(128)S(6)} %min_shard_map.3, s32[1024]{0:T(1024)S(1)} %pad_clamp_fusion), kind=kCustom, calls=%fused_computation.6 | custom fusion | flops 262144 | bytes 4462600 | tf_op jit(solution)/shard_map/scatter | solution.py:32
  312.5 0.0 copy-done
  312.5 0.0 copy-start.1
  312.5 0.0 copy-done.4
  312.5 0.0 copy-done.5
  312.6 1.4 divide_subtract_fusion
  (7 shorter events, 0.0 us)
Async XLA Ops:
  7.2 0.7 copy-start.6
  7.2 288.3 %all-reduce.2.cloned.1.call-start = ((), (), s32[]{:S(2)}) async-start(), calls=%async_computation | async-start | bytes 16777216 | tf_op jit(solution)/shard_map/psum | solution.py:16
  7.9 0.9 copy-start.3
  7.9 83.0 %copy-start.7 = (s32[512]{0:T(512)S(1)}, s32[512]{0:T(512)}, u32[]{:S(2)}) copy-start(s32[512]{0:T(512)} %param.12) | copy-start | bytes 6148
  306.4 2.5 copy-start.2
  308.9 3.7 %copy-start = (f32[4096]{0:T(1024)}, f32[4096]{0:T(1024)S(1)}, u32[]{:S(2)}) copy-start(f32[4096]{0:T(1024)S(1)} %scatter_fusion) | copy-start | bytes 49156
  308.9 3.7 %copy-start.4 = (f32[8,1024]{1,0:T(8,128)S(1)}, f32[8,1024]{1,0:T(8,128)}, u32[]{:S(2)}) copy-start(f32[8,1024]{1,0:T(8,128)} %param.8) | copy-start | bytes 98308
  308.9 3.7 %copy-start.5 = (f32[8,1024]{1,0:T(8,128)S(1)}, f32[8,1024]{1,0:T(8,128)}, u32[]{:S(2)}) copy-start(f32[8,1024]{1,0:T(8,128)} %param.9) | copy-start | bytes 98308
  312.5 1.5 copy-start.1
Sparse Core Ops, SparseCore 0:
  13.4 281.9 all-reduce.1
where the time goes:
time: 322 us; the launch traced here: 321 us
  waiting for transfers between devices  201 us (62%)
  blocking collectives  81.4 us (25%)
  between operations  15.5 us (5%)
  other arithmetic  15.3 us (5%)
  local copies, waits for them, and re-layouts  7.25 us (2%)
    psum x1, waiting for transfers between devices, body(): summed, embed_total = lax.psum((local_grad, embed_square), ('gx', 'gy'))  201 us
    psum x1, blocking collectives, body(): summed, embed_total = lax.psum((local_grad, embed_square), ('gx', 'gy'))  81.4 us
    reduce_sum x1, other arithmetic, body(): norm_sq = jnp.sum(mean_whole * mean_whole) + embed_total  9.38 us
  transfers between devices with their start and end apart: 1, of which 1 were waited for; matrix products, arithmetic and copies ran while one was open for 1% of the time, Pallas kernels for 0%

commit v1 on v0

--- a/solution.py
+++ b/solution.py
@@ -1,23 +1,417 @@
+import functools
+
 import jax
 import jax.numpy as jnp
 from jax import lax
+from jax.experimental import pallas as pl
+from jax.experimental.pallas import tpu as pltpu
 from jax.sharding import PartitionSpec as P
 
 learn_rate = 0.5
 max_norm = 8.0
 epsilon = 1e-10
 
+MESH = pl.DeviceIdType.MESH
+NX, NZ, NY, NC = 4, 8, 4, 2
+SHARDS = 256
+XS, YS, ZS = 3, 3, 2
+UNITS = XS + YS + ZS
+LANES = 128
+F32 = jnp.float32
+
+
+class Sends:
+    def __init__(self, send_sems, recv_sems):
+        self.send_sems, self.recv_sems = send_sems, recv_sems
+        self.made = {}
+
+    def start(self, name, src, dst, device):
+        slot = len(self.made)
+        copy = pltpu.make_async_remote_copy(
+            src_ref=src,
+            dst_ref=dst,
+            send_sem=self.send_sems.at[slot],
+            recv_sem=self.recv_sems.at[slot],
+            device_id=device,
+            device_id_type=MESH,
+        )
+        copy.start()
+        self.made[name] = copy
+
+    def wait(self, name):
+        self.made[name].wait_recv()
+
+    def drain(self):
+        for copy in self.made.values():
+            copy.wait_send()
+
+
+def reduce_kernel(
+    g_ref, e_ref, mean_ref, norm_ref,
+    acc, pair, emb,
+    a_relay, a_last, a_mid, a_end,
+    b_relay, b_last, b_mid, b_end,
+    c_far, c_chain, c_mid, c_end,
+    n_own, n_one, n_sum, n_two,
+    send_sems, recv_sems, load_sems,
+):
+    gx, gy = lax.axis_index("gx"), lax.axis_index("gy")
+    x, z = gx // NZ, gx % NZ
+    y, c = gy // NC, gy % NC
+
+    def dev(dx=0, dy=0, dz=0, core=None):
+        return (
+            ((x + dx) % NX) * NZ + (z + dz) % NZ,
+            ((y + dy) % NY) * NC + (c if core is None else core),
+        )
+
+    def dev_zc(k):
+        q = (z * NC + c + k) % (NZ * NC)
+        return (x * NZ + q // NC, y * NC + q % NC)
+
+    def dev_xy(k):
+        q = (x * NY + y + k) % (NX * NY)
+        return ((q // NY) * NZ + z, (q % NY) * NC + c)
+
+    cols = lambda u: pl.ds(u * LANES, LANES)
+    order = [0, 3, 6, 1, 4, 7, 2, 5]
+    loads = {}
+    for u in order:
+        loads[u] = pltpu.make_async_copy(
+            g_ref.at[:, :, :, c, :, cols(u)], acc.at[u], load_sems.at[u]
+        )
+        loads[u].start()
+    load_emb = pltpu.make_async_copy(e_ref, emb, load_sems.at[UNITS])
+    load_emb.start()
+
+    barrier = pltpu.get_barrier_semaphore()
+    for k in range(1, 16):
+        pl.semaphore_signal(barrier, inc=1, device_id=dev_zc(k), device_id_type=MESH)
+        pl.semaphore_signal(barrier, inc=1, device_id=dev_xy(k), device_id_type=MESH)
+    pl.semaphore_wait(barrier, 30)
+
+    net = Sends(send_sems, recv_sems)
+    other = 1 - c
+    mate = dev(core=other)
+
+    def part(ref, u, kind, k):
+        if kind == "x":
+            return ref.at[u, (x + k) % NX]
+        if kind == "y":
+            return ref.at[u, :, :, (y + k) % NY]
+        return ref.at[u, :, (z + k) % NZ]
+
+    def give(u, kind, k):
+        if kind == "x":
+            src = g_ref.at[(x + k) % NX, :, :, other, :, cols(u)]
+        elif kind == "y":
+            src = g_ref.at[:, :, (y + k) % NY, other, :, cols(u)]
+        else:
+            src = g_ref.at[:, (z + k) % NZ, :, other, :, cols(u)]
+        net.start(("pair", u, k), src, part(pair, u, kind, k), mate)
+
+    kinds = {u: "x" if u < XS else "y" if u < XS + YS else "z" for u in range(UNITS)}
+    waves = [[0, 3, 6], [1, 4, 7], [2, 5]]
+    far_of = {"x": [2], "y": [2], "z": [4]}
+    near_of = {"x": [1, 3, 0], "y": [1, 3, 0], "z": [3, 5, 2, 6, 1, 7, 0]}
+    for wave in waves:
+        for u in wave:
+            for k in far_of[kinds[u]]:
+                give(u, kinds[u], k)
+        for u in wave:
+            for k in near_of[kinds[u]]:
+                give(u, kinds[u], k)
+
+    def take(u, k):
+        kind = kinds[u]
+        net.wait(("pair", u, k))
+        mine = part(acc, u, kind, k)
+        mine[...] = mine[...] + part(pair, u, kind, k)[...]
+
+    loaded = set()
+
+    def load(u):
+        if u not in loaded:
+            loaded.add(u)
+            loads[u].wait()
+
+    LO, HI = pl.ds(0, 4), pl.ds(4, 4)
+
+    def a_part(u, k, half):
+        return acc.at[u, (x + k) % NX, half]
+
+    def a_far(w):
+        u = w
+        load(u)
+        take(u, 2)
+        net.start(("ar", w), a_part(u, 2, LO), a_relay.at[w, 0], dev(dx=1))
+        net.start(("al", w), a_part(u, 2, HI), a_relay.at[w, 1], dev(dx=-1))
+
+    def a_near(w):
+        u = w
+        take(u, 1)
+        net.start(("aer", w), a_part(u, 1, HI), a_last.at[w, 0, HI], dev(dx=1))
+        take(u, 3)
+        net.start(("ael", w), a_part(u, 3, LO), a_last.at[w, 1, LO], dev(dx=-1))
+        take(u, 0)
+
+    def a_late(w):
+        u = w
+        net.wait(("ar", w))
+        ref = a_part(u, 1, LO)
+        ref[...] = ref[...] + a_relay[w, 0]
+        net.start(("alr", w), ref, a_last.at[w, 0, LO], dev(dx=1))
+        net.wait(("al", w))
+        ref = a_part(u, 3, HI)
+        ref[...] = ref[...] + a_relay[w, 1]
+        net.start(("all", w), ref, a_last.at[w, 1, HI], dev(dx=-1))
+
+    def a_two(w):
+        u = w
+        for name in ("aer", "ael", "alr", "all"):
+            net.wait((name, w))
+        ref = acc.at[u, x]
+        ref[...] = ref[...] + (a_last[w, 0] + a_last[w, 1])
+        for k in (2, 1, 3):
+            net.start(("am", w, k), acc.at[u, x, :, (y + k) % NY], a_mid.at[w, k - 1], dev(dy=k))
+
+    def a_three(w):
+        u = w
+        for k in (1, 3, 2):
+            net.wait(("am", w, k))
+        ref = acc.at[u, x, :, y]
+        ref[...] = ref[...] + (a_mid[w, 0] + a_mid[w, 1] + a_mid[w, 2])
+        for k in (4, 3, 5, 2, 6, 1, 7):
+            net.start(("ae", w, k), acc.at[u, x, (z + k) % NZ, y], a_end.at[w, k - 1], dev(dz=k))
+
+    def b_part(u, k, half):
+        return acc.at[u, :, half, (y + k) % NY]
+
+    def b_far(w):
+        u = XS + w
+        load(u)
+        take(u, 2)
+        net.start(("br", w), b_part(u, 2, LO), b_relay.at[w, 0], dev(dy=1))
+        net.start(("bl", w), b_part(u, 2, HI), b_relay.at[w, 1], dev(dy=-1))
+
+    def b_near(w):
+        u = XS + w
+        take(u, 1)
+        net.start(("ber", w), b_part(u, 1, HI), b_last.at[w, 0, :, HI], dev(dy=1))
+        take(u, 3)
+        net.start(("bel", w), b_part(u, 3, LO), b_last.at[w, 1, :, LO], dev(dy=-1))
+        take(u, 0)
+
+    def b_late(w):
+        u = XS + w
+        net.wait(("br", w))
+        ref = b_part(u, 1, LO)
+        ref[...] = ref[...] + b_relay[w, 0]
+        net.start(("blr", w), ref, b_last.at[w, 0, :, LO], dev(dy=1))
+        net.wait(("bl", w))
+        ref = b_part(u, 3, HI)
+        ref[...] = ref[...] + b_relay[w, 1]
+        net.start(("bll", w), ref, b_last.at[w, 1, :, HI], dev(dy=-1))
+
+    def b_two(w):
+        u = XS + w
+        for name in ("ber", "bel", "blr", "bll"):
+            net.wait((name, w))
+        ref = acc.at[u, :, :, y]
+        ref[...] = ref[...] + (b_last[w, 0] + b_last[w, 1])
+        for k in (2, 1, 3):
+            net.start(("bm", w, k), acc.at[u, (x + k) % NX, :, y], b_mid.at[w, k - 1], dev(dx=k))
+
+    def b_three(w):
+        u = XS + w
+        for k in (1, 3, 2):
+            net.wait(("bm", w, k))
+        ref = acc.at[u, x, :, y]
+        ref[...] = ref[...] + (b_mid[w, 0] + b_mid[w, 1] + b_mid[w, 2])
+        for k in (4, 3, 5, 2, 6, 1, 7):
+            net.start(("be", w, k), acc.at[u, x, (z + k) % NZ, y], b_end.at[w, k - 1], dev(dz=k))
+
+    XLO, XHI = pl.ds(0, 2), pl.ds(2, 2)
+
+    def c_part(u, k, half=slice(None)):
+        return acc.at[u, half, (z + k) % NZ]
+
+    def c_zero(w):
+        u = XS + YS + w
+        load(u)
+        take(u, 4)
+        net.start(("c1r", w), c_part(u, 4, XLO), c_far.at[w, 0], dev(dz=1))
+        net.start(("c1l", w), c_part(u, 4, XHI), c_far.at[w, 1], dev(dz=-1))
+
+    def c_near(w):
+        u = XS + YS + w
+        take(u, 3)
+        net.start(("c2er", w), c_part(u, 3, XHI), c_chain.at[w, 0, 0, XHI], dev(dz=1))
+        take(u, 5)
+        net.start(("c2el", w), c_part(u, 5, XLO), c_chain.at[w, 1, 0, XLO], dev(dz=-1))
+        for k in (2, 6, 1, 7, 0):
+            take(u, k)
+
+    def c_one(w):
+        u = XS + YS + w
+        net.wait(("c1r", w))
+        ref = c_part(u, 3, XLO)
+        ref[...] = ref[...] + c_far[w, 0]
+        net.start(("c2lr", w), ref, c_chain.at[w, 0, 0, XLO], dev(dz=1))
+        net.wait(("c1l", w))
+        ref = c_part(u, 5, XHI)
+        ref[...] = ref[...] + c_far[w, 1]
+        net.start(("c2ll", w), ref, c_chain.at[w, 1, 0, XHI], dev(dz=-1))
+
+    def c_two(w):
+        u = XS + YS + w
+        net.wait(("c2er", w))
+        net.wait(("c2lr", w))
+        ref = c_part(u, 2)
+        ref[...] = ref[...] + c_chain[w, 0, 0]
+        net.start(("c3r", w), ref, c_chain.at[w, 0, 1], dev(dz=1))
+        net.wait(("c2el", w))
+        net.wait(("c2ll", w))
+        ref = c_part(u, 6)
+        ref[...] = ref[...] + c_chain[w, 1, 0]
+        net.start(("c3l", w), ref, c_chain.at[w, 1, 1], dev(dz=-1))
+
+    def c_three(w):
+        u = XS + YS + w
+        net.wait(("c3r", w))
+        ref = c_part(u, 1)
+        ref[...] = ref[...] + c_chain[w, 0, 1]
+        net.start(("c4r", w), ref, c_chain.at[w, 0, 2], dev(dz=1))
+        net.wait(("c3l", w))
+        ref = c_part(u, 7)
+        ref[...] = ref[...] + c_chain[w, 1, 1]
+        net.start(("c4l", w), ref, c_chain.at[w, 1, 2], dev(dz=-1))
+
+    def c_four(w):
+        u = XS + YS + w
+        net.wait(("c4r", w))
+        net.wait(("c4l", w))
+        ref = acc.at[u, :, z]
+        ref[...] = ref[...] + (c_chain[w, 0, 2] + c_chain[w, 1, 2])
+        for k in (2, 1, 3):
+            net.start(("cm", w, k), acc.at[u, (x + k) % NX, z], c_mid.at[w, k - 1], dev(dx=k))
+
+    def c_five(w):
+        u = XS + YS + w
+        for k in (1, 3, 2):
+            net.wait(("cm", w, k))
+        ref = acc.at[u, x, z]
+        ref[...] = ref[...] + (c_mid[w, 0] + c_mid[w, 1] + c_mid[w, 2])
+        for k in (2, 1, 3):
+            net.start(("ce", w, k), acc.at[u, x, z, (y + k) % NY], c_end.at[w, k - 1], dev(dy=k))
+
+    squares = []
+
+    def end(u, name, w, ends, ks):
+        total = acc[u, x, z, y]
+        for k in ks:
+            net.wait((name, w, k))
+            total = total + ends[w, k - 1]
+        mean = total / F32(SHARDS)
+        mean_ref[:, cols(u)] = mean
+        squares.append(mean * mean)
+
+    def a_end_step(w):
+        end(w, "ae", w, a_end, (1, 7, 2, 6, 3, 5, 4))
+
+    def b_end_step(w):
+        end(XS + w, "be", w, b_end, (1, 7, 2, 6, 3, 5, 4))
+
+    def c_end_step(w):
+        end(XS + YS + w, "ce", w, c_end, (1, 3, 2))
+
+    a_far(0); b_far(0); c_zero(0)
+    a_near(0); b_near(0); c_near(0)
+    a_far(1); b_far(1); c_zero(1)
+    c_one(0); a_late(0); b_late(0)
+    a_near(1); b_near(1); c_near(1)
+    a_far(2); b_far(2)
+    load_emb.wait()
+    grads = emb[...]
+    squares.append(jnp.sum((grads * grads).reshape(-1, 8, LANES), axis=0))
+    c_two(0)
+    c_one(1)
+    a_late(1); b_late(1)
+    a_near(2); b_near(2)
+    a_two(0); b_two(0)
+    c_three(0); c_two(1)
+    a_late(2); b_late(2)
+    a_two(1); b_two(1)
+    a_three(0); b_three(0)
+    c_four(0); c_three(1)
+    a_three(1); b_three(1)
+    a_end_step(0); b_end_step(0)
+    a_two(2); b_two(2)
+    c_five(0); c_four(1)
+    c_end_step(0)
+    a_end_step(1); b_end_step(1)
+    a_three(2); b_three(2)
+    c_five(1)
+    c_end_step(1)
+    a_end_step(2); b_end_step(2)
+
+    total = functools.reduce(lambda p, q: p + q, squares)
+    n_own[...] = jnp.sum(total, axis=0, keepdims=True)
+    for k in range(1, 16):
+        net.start(("n1", k), n_own, n_one.at[k - 1], dev_zc(k))
+    line = n_own[...]
+    for k in range(1, 16):
+        net.wait(("n1", k))
+    for k in range(1, 16):
+        line = line + n_one[k - 1]
+    n_sum[...] = line
+    for k in range(1, 16):
+        net.start(("n2", k), n_sum, n_two.at[k - 1], dev_xy(k))
+    for k in range(1, 16):
+        net.wait(("n2", k))
+    for k in range(1, 16):
+        line = line + n_two[k - 1]
+    norm_ref[...] = line
+    net.drain()
+
+
+def reduce_mean(grads, emb):
+    vm = lambda *shape: pltpu.VMEM(shape + (8, LANES), F32)
+    row = lambda *shape: pltpu.VMEM(shape + (1, LANES), F32)
+    copies = 4 * (XS + YS) + 8 * ZS + 16 * (XS + YS) + 16 * ZS + 30
+    return pl.pallas_call(
+        reduce_kernel,
+        name="reduce_mean",
+        out_shape=(
+            jax.ShapeDtypeStruct((8, 1024), F32),
+            jax.ShapeDtypeStruct((1, LANES), F32),
+        ),
+        in_specs=[pl.BlockSpec(memory_space=pl.ANY)] * 2,
+        out_specs=(
+            pl.BlockSpec(memory_space=pltpu.VMEM),
+            pl.BlockSpec(memory_space=pltpu.VMEM),
+        ),
+        scratch_shapes=[
+            vm(UNITS, NX, NZ, NY),
+            vm(UNITS, NX, NZ, NY),
+            pltpu.VMEM(emb.shape, F32),
+            vm(XS, 2, 4, NY), vm(XS, 2, NZ, NY), vm(XS, 3, NZ), vm(XS, 7),
+            vm(YS, 2, NX, 4), vm(YS, 2, NX, NZ), vm(YS, 3, NZ), vm(YS, 7),
+            vm(ZS, 2, 2, NY), vm(ZS, 2, 3, NX, NY), vm(ZS, 3, NY), vm(ZS, 3),
+            row(), row(15), row(), row(15),
+            pltpu.SemaphoreType.DMA((copies,)),
+            pltpu.SemaphoreType.DMA((copies,)),
+            pltpu.SemaphoreType.DMA((UNITS + 1,)),
+        ],
+        compiler_params=pltpu.CompilerParams(
+            collective_id=0, has_side_effects=True, vmem_limit_bytes=24 * 1024 * 1024
+        ),
+    )(grads.reshape(NX, NZ, NY, NC, 8, 1024), emb)
+
 
 def body(dense_grads, dense_param, dense_acc, table, row_acc, touched, emb_grads):
-    shards = lax.axis_size(("gx", "gy"))
-    local_grad = dense_grads[0]
-    embed_square = jnp.sum(emb_grads * emb_grads)
-    own_rows = dense_param.shape[0]
-    summed, embed_total = lax.psum((local_grad, embed_square), ("gx", "gy"))
-    mean_whole = summed / jnp.float32(shards)
-    norm_sq = jnp.sum(mean_whole * mean_whole) + embed_total
-    start = lax.axis_index(("gx", "gy")) * own_rows
-    mean_grad = lax.dynamic_slice_in_dim(mean_whole, start, own_rows, 0)
+    mean_grad, norm_line = reduce_mean(dense_grads, emb_grads)
+    norm_sq = jnp.sum(norm_line)
     clip = jnp.minimum(jnp.float32(1.0), max_norm / (jnp.sqrt(norm_sq) + 1e-06))
     scaled = clip * mean_grad
     new_dense_acc = dense_acc + scaled * scaled

time: 322 us -> 71.1 us (0.22)
  waiting for transfers between devices: 201 us -> 0 us
  blocking collectives: 81.4 us -> 0 us
  Pallas kernels: 0 us -> 53.9 us
  between operations: 15.5 us -> 1.49 us
  other arithmetic: 15.3 us -> 5.02 us
    psum x1 -> x0, waiting for transfers between devices: 201 us -> none  [body(): summed, embed_total = lax.psum((local_grad, embed_square), ('gx', 'gy'))]
    psum x1 -> x0, blocking collectives: 81.4 us -> none  [body(): summed, embed_total = lax.psum((local_grad, embed_square), ('gx', 'gy'))]
    pallas_call x0 -> x1, Pallas kernels: none -> 53.9 us  [reduce_mean(): pl.pallas_call(reduce_kernel, name='reduce_mean', out_shape=(jax.ShapeDty...]
    reduce_sum x2 -> x1, other arithmetic: 10 us -> 0.6 us  [body(): norm_sq = jnp.sum(norm_line)]
  transfers between devices with their start and end apart: 1 -> 0, of which waited for: 1 -> 0; matrix products, arithmetic and copies ran while one was open for 1% -> 0% of each run, Pallas kernels for 0% -> 0%
where the time goes in v1:
time: 71.1 us; the launch traced here: 70.9 us
  Pallas kernels  53.9 us (76%)
  local copies, waits for them, and re-layouts  10.4 us (15%)
  other arithmetic  5.02 us (7%)
  between operations  1.49 us (2%)
    pallas_call x1, Pallas kernels, reduce_mean(): pl.pallas_call(reduce_kernel, name='reduce_mean', out_shape=(jax.ShapeDty...  53.9 us
    unnamed x17, local copies, waits for them, and re-layouts  4.81 us
    scatter x1, other arithmetic, body(): new_table = table.at[touched].set(updated_rows)  3.6 us
    gather x1, local copies, waits for them, and re-layouts, body(): updated_acc = row_acc[touched] + square_mean  3.14 us
    scatter x1, local copies, waits for them, and re-layouts, body(): new_row_acc = row_acc.at[touched].set(updated_acc)  2.48 us

profile of v1, /device:TPU:1, one launch (start us, length us, event | category | flops | bytes accessed | tf_op | source)
XLA Modules:
  0.0 70.9 jit_solution(2105978390280135338)
XLA Ops:
  0.6 0.7 %copy.16 = f32[4096]{0:T(1024)S(1)} copy(f32[4096]{0:T(1024)} %param.11) | data formatting | bytes 32768
  1.4 0.0 copy-start.7
  1.4 0.7 copy-done.7
  2.0 0.0 copy-start.1
  2.0 3.1 %gather_fusion = f32[512]{0:T(512)S(1)} fusion(f32[4096]{0:T(1024)S(1)} %copy.16, s32[1024]{0:T(1024)S(1)} %pad_clamp_fusion), kind=kCustom, calls=%fused_computation.1 | custom fusion | bytes 6144 | tf_op jit(solution)/shard_map/gather | solution.py:421
  5.2 0.0 copy-done.1
  5.2 0.0 copy-start
  5.2 3.4 %copy-done = f32[1,2048,1024]{2,1,0:T(8,128)S(1)} copy-done((f32[1,2048,1024]{2,1,0:T(8,128)S(1)}, f32[1,2048,1024]{2,1,0:T(8,128)}, u32[]{:S(2)}) %copy-start) | copy-done | bytes 8388632
  8.6 0.0 copy-start.4
  8.6 53.9 %reduce_mean.1 = (f32[8,1024]{1,0:T(8,128)S(1)}, f32[1,128]{1,0:T(1,128)S(1)}) custom-call(f32[4,8,4,2,8,1024]{5,4,3,2,1,0:T(8,128)S(1)} %bitcast.1, f32[512,128]{1,0:T(8,128)S(1)} %copy-done.1), custom_call_target="tpu_custom_call" | custom-call | tf_op jit(solution)/shard_map/reduce_mean/pallas_call | solution.py:382
  62.5 0.6 reduce_sum.18
  63.9 0.1 multiply_reduce_fusion
  64.0 0.0 copy-done.4
  64.1 3.6 %scatter_custom_fusion = f32[4096,128]{1,0:T(8,128)S(1)} fusion(f32[4096,128]{1,0:T(8,128)S(1)} %copy-done.4, s32[512]{0:T(512)S(1)} %compare_select_fusion, f32[512,128]{1,0:T(8,128)S(1)} %copy-done.1, f32[512]{0:T(512)S(1)} %get-tuple-element.8, f32[]{:T(128)} %constant.3.clone.1, f32[]{:T(128)S(6)} %min_shard_map.3, s32[1024]{0:T(1024)S(1)} %pad_clamp_fusion), kind=kCustom, calls=%fused_computation.4 | custom fusion | flops 262144 | bytes 4462600 | tf_op jit(solution)/shard_map/scatter | solution.py:426
  67.7 0.0 copy-start.3
  67.7 0.0 copy-start.5
  67.7 0.0 copy-start.6
  67.7 2.5 %scatter_fusion = f32[4096]{0:T(1024)S(1)} fusion(f32[4096]{0:T(1024)S(1)} %copy.16, s32[512]{0:T(512)S(1)} %compare_select_fusion, f32[512]{0:T(512)S(1)} %get-tuple-element.9), kind=kCustom, calls=%fused_computation.3 | custom fusion | bytes 8192 | tf_op jit(solution)/shard_map/scatter | solution.py:422
  70.2 0.0 copy-done.3
  70.2 0.0 copy-start.2
  70.2 0.0 copy-done.5
  70.2 0.0 copy-done.6
  70.2 0.6 divide_subtract_fusion
  70.9 0.0 copy-done.2
  (3 shorter events, 0.0 us)
Async XLA Ops:
  1.4 0.7 copy-start.7
  2.0 3.2 %copy-start.1 = (f32[512,128]{1,0:T(8,128)S(1)}, f32[512,128]{1,0:T(8,128)}, u32[]{:S(2)}) copy-start(f32[512,128]{1,0:T(8,128)} %e_ref.1) | copy-start | bytes 786436
  5.2 3.4 %copy-start = (f32[1,2048,1024]{2,1,0:T(8,128)S(1)}, f32[1,2048,1024]{2,1,0:T(8,128)}, u32[]{:S(2)}) copy-start(f32[1,2048,1024]{2,1,0:T(8,128)} %param.7) | copy-start | bytes 25165828
  8.6 55.5 %copy-start.4 = (f32[4096,128]{1,0:T(8,128)S(1)}, f32[4096,128]{1,0:T(8,128)}, u32[]{:S(2)}) copy-start(f32[4096,128]{1,0:T(8,128)} %param.10) | copy-start | bytes 6291460
  67.7 2.5 %copy-start.3 = (f32[4096,128]{1,0:T(8,128)}, f32[4096,128]{1,0:T(8,128)S(1)}, u32[]{:S(2)}) copy-start(f32[4096,128]{1,0:T(8,128)S(1)} %scatter_custom_fusion) | copy-start | bytes 6291460
  67.7 2.5 %copy-start.5 = (f32[8,1024]{1,0:T(8,128)S(1)}, f32[8,1024]{1,0:T(8,128)}, u32[]{:S(2)}) copy-start(f32[8,1024]{1,0:T(8,128)} %param.8) | copy-start | bytes 98308
  67.7 2.5 %copy-start.6 = (f32[8,1024]{1,0:T(8,128)S(1)}, f32[8,1024]{1,0:T(8,128)}, u32[]{:S(2)}) copy-start(f32[8,1024]{1,0:T(8,128)} %param.9) | copy-start | bytes 98308
  70.2 0.7 copy-start.2

commit v2 on v1

--- a/solution.py
+++ b/solution.py
@@ -47,8 +47,9 @@
 
 
 def reduce_kernel(
-    g_ref, e_ref, mean_ref, norm_ref,
-    acc, pair, emb,
+    g_ref, e_ref, table_ref, row_acc_ref, touched_ref,
+    mean_ref, norm_ref, tab, emb, row_tab, row_sq, row_ra, flat_sq,
+    acc, pair, idx, ra,
     a_relay, a_last, a_mid, a_end,
     b_relay, b_last, b_mid, b_end,
     c_far, c_chain, c_mid, c_end,
@@ -81,8 +82,14 @@
             g_ref.at[:, :, :, c, :, cols(u)], acc.at[u], load_sems.at[u]
         )
         loads[u].start()
-    load_emb = pltpu.make_async_copy(e_ref, emb, load_sems.at[UNITS])
-    load_emb.start()
+    prep_loads = [
+        pltpu.make_async_copy(src, dst, load_sems.at[UNITS + i])
+        for i, (src, dst) in enumerate(
+            ((e_ref, emb), (touched_ref, idx), (row_acc_ref, ra), (table_ref, tab))
+        )
+    ]
+    for copy in prep_loads:
+        copy.start()
 
     barrier = pltpu.get_barrier_semaphore()
     for k in range(1, 16):
@@ -307,6 +314,34 @@
 
     squares = []
 
+    def prep_start():
+        for copy in prep_loads:
+            copy.wait()
+        grads = emb[...]
+        own = grads * grads
+        squares.append(jnp.sum(own.reshape(-1, 8, LANES), axis=0))
+        mean = jnp.sum(own, axis=1, keepdims=True) / F32(LANES)
+        row_sq[...] = jnp.broadcast_to(mean, row_sq.shape)
+
+    spot = lax.broadcasted_iota(jnp.int32, (32, LANES), 0) * LANES
+    spot = spot + lax.broadcasted_iota(jnp.int32, (32, LANES), 1)
+    flat = [jnp.zeros((32, LANES), F32)]
+
+    def prep(part, parts=8):
+        size = 512 // parts
+
+        def eight(i, total):
+            base = part * size + i * 8
+            for j in range(8):
+                t = base + j
+                r = idx[t]
+                row_tab[pl.ds(t, 1), :] = tab[pl.ds(r, 1), :]
+                row_ra[pl.ds(t, 1), :] = jnp.full((1, LANES), ra[r], F32)
+                total = jnp.where(spot == r, row_sq[pl.ds(t, 1), :], total)
+            return total
+
+        flat[0] = lax.fori_loop(0, size // 8, eight, flat[0])
+
     def end(u, name, w, ends, ks):
         total = acc[u, x, z, y]
         for k in ks:
@@ -331,27 +366,34 @@
     c_one(0); a_late(0); b_late(0)
     a_near(1); b_near(1); c_near(1)
     a_far(2); b_far(2)
-    load_emb.wait()
-    grads = emb[...]
-    squares.append(jnp.sum((grads * grads).reshape(-1, 8, LANES), axis=0))
+    prep_start()
     c_two(0)
     c_one(1)
     a_late(1); b_late(1)
     a_near(2); b_near(2)
+    prep(0)
     a_two(0); b_two(0)
+    prep(1)
     c_three(0); c_two(1)
     a_late(2); b_late(2)
     a_two(1); b_two(1)
+    prep(2)
     a_three(0); b_three(0)
+    prep(3)
     c_four(0); c_three(1)
     a_three(1); b_three(1)
+    prep(4)
     a_end_step(0); b_end_step(0)
     a_two(2); b_two(2)
     c_five(0); c_four(1)
+    prep(5)
     c_end_step(0)
+    prep(6)
     a_end_step(1); b_end_step(1)
     a_three(2); b_three(2)
     c_five(1)
+    prep(7)
+    flat_sq[...] = flat[0]
     c_end_step(1)
     a_end_step(2); b_end_step(2)
 
@@ -375,56 +417,107 @@
     net.drain()
 
 
-def reduce_mean(grads, emb):
+def reduce_mean(grads, emb, table, row_acc, touched):
     vm = lambda *shape: pltpu.VMEM(shape + (8, LANES), F32)
     row = lambda *shape: pltpu.VMEM(shape + (1, LANES), F32)
     copies = 4 * (XS + YS) + 8 * ZS + 16 * (XS + YS) + 16 * ZS + 30
+    shapes = ((8, 1024), (1, LANES), table.shape) + (emb.shape,) * 4 + ((32, LANES),)
     return pl.pallas_call(
         reduce_kernel,
         name="reduce_mean",
-        out_shape=(
-            jax.ShapeDtypeStruct((8, 1024), F32),
-            jax.ShapeDtypeStruct((1, LANES), F32),
-        ),
-        in_specs=[pl.BlockSpec(memory_space=pl.ANY)] * 2,
-        out_specs=(
-            pl.BlockSpec(memory_space=pltpu.VMEM),
-            pl.BlockSpec(memory_space=pltpu.VMEM),
-        ),
+        out_shape=[jax.ShapeDtypeStruct(shape, F32) for shape in shapes],
+        in_specs=[pl.BlockSpec(memory_space=pltpu.HBM)] * 5,
+        out_specs=[pl.BlockSpec(memory_space=pltpu.VMEM)] * len(shapes),
         scratch_shapes=[
             vm(UNITS, NX, NZ, NY),
             vm(UNITS, NX, NZ, NY),
-            pltpu.VMEM(emb.shape, F32),
+            pltpu.SMEM(touched.shape, jnp.int32),
+            pltpu.SMEM(row_acc.shape, F32),
             vm(XS, 2, 4, NY), vm(XS, 2, NZ, NY), vm(XS, 3, NZ), vm(XS, 7),
             vm(YS, 2, NX, 4), vm(YS, 2, NX, NZ), vm(YS, 3, NZ), vm(YS, 7),
             vm(ZS, 2, 2, NY), vm(ZS, 2, 3, NX, NY), vm(ZS, 3, NY), vm(ZS, 3),
             row(), row(15), row(), row(15),
             pltpu.SemaphoreType.DMA((copies,)),
             pltpu.SemaphoreType.DMA((copies,)),
-            pltpu.SemaphoreType.DMA((UNITS + 1,)),
+            pltpu.SemaphoreType.DMA((UNITS + 4,)),
         ],
         compiler_params=pltpu.CompilerParams(
-            collective_id=0, has_side_effects=True, vmem_limit_bytes=24 * 1024 * 1024
+            collective_id=0, has_side_effects=True, vmem_limit_bytes=50 * 1024 * 1024
         ),
-    )(grads.reshape(NX, NZ, NY, NC, 8, 1024), emb)
+    )(grads.reshape(NX, NZ, NY, NC, 8, 1024), emb, table, row_acc, touched)
+
+
+def update_kernel(
+    norm_ref, mean_ref, tab_ref, emb_ref, row_tab, row_sq, row_ra, flat_sq,
+    param_ref, acc_ref, ra_ref, touched_ref,
+    dense_out, dense_acc_out, table_out, row_acc_out, tab,
+    idx, rows, dense_new, dense_acc_new, ra_new, sems,
+):
+    load = pltpu.make_async_copy(touched_ref, idx, sems.at[0])
+    load.start()
+    norm_sq = jnp.sum(norm_ref[...], axis=1, keepdims=True)
+    clip = jnp.minimum(F32(1.0), F32(max_norm) / (jnp.sqrt(norm_sq) + F32(1e-06)))
+    square = clip * clip
+    live = clip > 0.0
+
+    def grown(old, mean_square):
+        return old + jnp.where(live, square * mean_square, 0.0)
+
+    new_ra = grown(row_ra[...], row_sq[...])
+    step = (F32(learn_rate) * clip) * emb_ref[...] / (jnp.sqrt(new_ra) + F32(epsilon))
+    rows[...] = row_tab[...] - step
+    load.wait()
+
+    def sixteen(i, carry):
+        for j in range(16):
+            t = i * 16 + j
+            tab[pl.ds(idx[t], 1), :] = rows[pl.ds(t, 1), :]
+        return carry
+
+    lax.fori_loop(0, 32, sixteen, 0)
+    out = [pltpu.make_async_copy(tab, table_out, sems.at[1])]
+    out[0].start()
+    ra_new[...] = grown(ra_ref[...], flat_sq[...])
+    scaled = clip * mean_ref[...]
+    grow = acc_ref[...] + scaled * scaled
+    dense_acc_new[...] = grow
+    dense_new[...] = param_ref[...] - F32(learn_rate) * scaled / (jnp.sqrt(grow) + F32(epsilon))
+    for i, (src, dst) in enumerate(
+        ((ra_new, row_acc_out), (dense_acc_new, dense_acc_out), (dense_new, dense_out))
+    ):
+        out.append(pltpu.make_async_copy(src, dst, sems.at[2 + i]))
+        out[-1].start()
+    for copy in out:
+        copy.wait()
 
 
 def body(dense_grads, dense_param, dense_acc, table, row_acc, touched, emb_grads):
-    mean_grad, norm_line = reduce_mean(dense_grads, emb_grads)
-    norm_sq = jnp.sum(norm_line)
-    clip = jnp.minimum(jnp.float32(1.0), max_norm / (jnp.sqrt(norm_sq) + 1e-06))
-    scaled = clip * mean_grad
-    new_dense_acc = dense_acc + scaled * scaled
-    new_dense = dense_param - learn_rate * scaled / (jnp.sqrt(new_dense_acc) + epsilon)
-    row_grads = clip * emb_grads
-    square_mean = jnp.mean(row_grads * row_grads, axis=1)
-    updated_acc = row_acc[touched] + square_mean
-    new_row_acc = row_acc.at[touched].set(updated_acc)
-    updated_rows = (
-        table[touched] - learn_rate * row_grads / (jnp.sqrt(updated_acc) + epsilon)[:, None]
+    mean, norm, tab, emb, row_tab, row_sq, row_ra, flat_sq = reduce_mean(
+        dense_grads, emb_grads, table, row_acc, touched
     )
-    new_table = table.at[touched].set(updated_rows)
-    return (new_dense, new_dense_acc, new_table, new_row_acc)
+    vmem, hbm = pl.BlockSpec(memory_space=pltpu.VMEM), pl.BlockSpec(memory_space=pltpu.HBM)
+    shapes = (dense_param.shape, dense_param.shape, table.shape, (32, LANES), table.shape)
+    new_dense, new_dense_acc, new_table, new_row_acc, _ = pl.pallas_call(
+        update_kernel,
+        name="update",
+        out_shape=[jax.ShapeDtypeStruct(shape, F32) for shape in shapes],
+        in_specs=[vmem] * 11 + [hbm],
+        out_specs=[hbm] * 4 + [vmem],
+        scratch_shapes=[
+            pltpu.SMEM(touched.shape, jnp.int32),
+            pltpu.VMEM(emb.shape, F32),
+            pltpu.VMEM(dense_param.shape, F32),
+            pltpu.VMEM(dense_param.shape, F32),
+            pltpu.VMEM((32, LANES), F32),
+            pltpu.SemaphoreType.DMA((5,)),
+        ],
+        input_output_aliases={2: 4},
+        compiler_params=pltpu.CompilerParams(vmem_limit_bytes=16 * 1024 * 1024),
+    )(
+        norm, mean, tab, emb, row_tab, row_sq, row_ra, flat_sq,
+        dense_param, dense_acc, row_acc.reshape(32, LANES), touched,
+    )
+    return (new_dense, new_dense_acc, new_table, new_row_acc.reshape(-1))
 
 
 def solution(mesh):

time: 71.1 us -> 59.4 us (0.84)
  local copies, waits for them, and re-layouts: 10.4 us -> 2.35 us
  other arithmetic: 5.02 us -> 0 us
  Pallas kernels: 53.9 us -> 56.2 us
  between operations: 1.49 us -> 0.67 us
    scatter x1 -> x0, other arithmetic: 3.6 us -> none  [body(): new_table = table.at[touched].set(updated_rows)]
    gather x1 -> x0, local copies, waits for them, and re-layouts: 3.14 us -> none  [body(): updated_acc = row_acc[touched] + square_mean]
    scatter x1 -> x0, local copies, waits for them, and re-layouts: 2.48 us -> none  [body(): new_row_acc = row_acc.at[touched].set(updated_acc)]
    unnamed x17 -> x10, local copies, waits for them, and re-layouts: 4.81 us -> 2.35 us
    pallas_call x1 -> x2, Pallas kernels: 53.9 us -> 56.2 us  [the longest x1 53.7 us: reduce_mean(): pl.pallas_call(reduce_kernel, name='reduce_mean', out_shape=[jax.ShapeDty...]
    reduce_sum x2 -> x0, other arithmetic: 0.75 us -> none  [the longest x1 0.6 us: body(): norm_sq = jnp.sum(norm_line)]
where the time goes in v2:
time: 59.4 us; the launch traced here: 59.2 us
  Pallas kernels  56.2 us (95%)
  local copies, waits for them, and re-layouts  2.35 us (4%)
  between operations  0.67 us (1%)
    pallas_call x1, Pallas kernels, reduce_mean(): pl.pallas_call(reduce_kernel, name='reduce_mean', out_shape=[jax.ShapeDty...  53.7 us
    pallas_call x1, Pallas kernels, body(): pl.pallas_call(update_kernel, name='update', out_shape=[jax.ShapeDtypeStr...  2.49 us
    unnamed x10, local copies, waits for them, and re-layouts  2.35 us

profile of v2, /device:TPU:1, one launch (start us, length us, event | category | flops | bytes accessed | tf_op | source)
XLA Modules:
  0.0 59.2 jit_solution(15019105697232305781)
XLA Ops:
  0.6 0.0 copy-start
  0.6 0.9 %copy-done = f32[512,128]{1,0:T(8,128)S(1)} copy-done((f32[512,128]{1,0:T(8,128)S(1)}, f32[512,128]{1,0:T(8,128)}, u32[]{:S(2)}) %copy-start) | copy-done | bytes 262168
  1.6 0.0 copy-start.1
  1.6 0.7 %copy-done.1 = f32[4096]{0:T(1024)S(1)} copy-done((f32[4096]{0:T(1024)S(1)}, f32[4096]{0:T(1024)}, u32[]{:S(2)}) %copy-start.1) | copy-done | bytes 16408
  2.3 0.0 copy-start.4
  2.3 0.7 %copy-done.4 = s32[512]{0:T(512)S(1)} copy-done((s32[512]{0:T(512)S(1)}, s32[512]{0:T(512)}, u32[]{:S(2)}) %copy-start.4) | copy-done | bytes 2072
  3.0 0.0 copy-start.2
  3.0 0.0 copy-start.3
  3.0 53.7 %reduce_mean.1 = (f32[8,1024]{1,0:T(8,128)S(1)}, f32[1,128]{1,0:T(1,128)S(1)}, f32[4096,128]{1,0:T(8,128)S(1)}, f32[512,128]{1,0:T(8,128)S(1)}, f32[512,128]{1,0...) custom-call(f32[4,8,4,2,8,1024]{5,4,3,2,1,0:T(8,128)} %bitcast.4, ...), custom_call_target="tpu_custom_call" | custom-call | tf_op jit(solution)/shard_map/reduce_mean/pallas_call | solution.py:425
  56.7 0.0 copy-done.2
  56.7 0.0 copy-done.3
  56.7 2.5 %update.1 = (f32[8,1024]{1,0:T(8,128)}, f32[8,1024]{1,0:T(8,128)}, f32[4096,128]{1,0:T(8,128)}, f32[32,128]{1,0:T(8,128)}, f32[4096,128]{1,0:T(8,128)S(1)}) custom-call(f32[1,128]{1,0:T(1,128)S(1)} %get-tuple-element.16.norm_ref, f32[8,1024]{1,0:T(8,128)S(1)} %get-tuple-element.17.mean_ref, ...), custom_call_target="tpu_custom_call", output_to_operand_aliasing={{4}: (2, {})} | custom-call | tf_op jit(solution)/shard_map/update/pallas_call | solution.py:500
Async XLA Ops:
  0.6 1.0 %copy-start = (f32[512,128]{1,0:T(8,128)S(1)}, f32[512,128]{1,0:T(8,128)}, u32[]{:S(2)}) copy-start(f32[512,128]{1,0:T(8,128)} %e_ref.1) | copy-start | bytes 786436
  1.6 0.7 %copy-start.1 = (f32[4096]{0:T(1024)S(1)}, f32[4096]{0:T(1024)}, u32[]{:S(2)}) copy-start(f32[4096]{0:T(1024)} %row_acc_ref.1) | copy-start | bytes 49156
  2.3 0.7 %copy-start.4 = (s32[512]{0:T(512)S(1)}, s32[512]{0:T(512)}, u32[]{:S(2)}) copy-start(s32[512]{0:T(512)} %touched_ref.3) | copy-start | bytes 6148
  3.0 53.7 %copy-start.2 = (f32[8,1024]{1,0:T(8,128)S(1)}, f32[8,1024]{1,0:T(8,128)}, u32[]{:S(2)}) copy-start(f32[8,1024]{1,0:T(8,128)} %param_ref.1) | copy-start | bytes 98308
  3.0 53.7 %copy-start.3 = (f32[8,1024]{1,0:T(8,128)S(1)}, f32[8,1024]{1,0:T(8,128)}, u32[]{:S(2)}) copy-start(f32[8,1024]{1,0:T(8,128)} %acc_ref.1) | copy-start | bytes 98308

commit v3 on v0

v3 whole, which is shorter than its diff:
```python
import functools

import jax
import jax.numpy as jnp
from jax import lax
from jax.experimental import pallas as pl
from jax.experimental.pallas import tpu as pltpu
from jax.sharding import PartitionSpec as P

learn_rate = 0.5
max_norm = 8.0
epsilon = 1e-10

MESH = pl.DeviceIdType.MESH
NX, NZ, NY, NC = 4, 8, 4, 2
SHARDS = 256
XS, YS, ZS = 3, 3, 2
UNITS = XS + YS + ZS
LANES = 128
SEMS = 88
F32 = jnp.float32


PLANE = sorted(
    [(dx, dy) for dx in range(NX) for dy in range(NY) if dx or dy],
    key=lambda d: -(min(d[0], NX - d[0]) + min(d[1], NY - d[1])),
)


def far(k):
    dx, dz, dy = k // (NZ * NY * NC), k // (NY * NC) % NZ, k // NC % NY
    return min(dx, NX - dx) + min(dz, NZ - dz) + min(dy, NY - dy)


RANKS = sorted(range(1, SHARDS), key=lambda k: -far(k))


class Net:
    def __init__(self, sems, mate):
        self.sems, self.mate = sems, mate
        self.slots, self.sent = {}, {}

    def sem(self, name):
        return self.sems.at[self.slots.setdefault(name, len(self.slots))]

    def start(self, name, whole, src, dst, device):
        self.sent[name[0]] = whole
        pltpu.make_async_remote_copy(
            src_ref=src,
            dst_ref=dst,
            send_sem=self.sem(("sent", name[0])),
            recv_sem=self.sem(name),
            device_id=device,
            device_id_type=MESH,
        ).start()

    def filled(self, ref, recv, sent):
        return pltpu.make_async_remote_copy(
            src_ref=ref,
            dst_ref=ref,
            send_sem=self.sem(sent),
            recv_sem=self.sem(recv),
            device_id=self.mate,
            device_id_type=MESH,
        )

    def wait(self, name, ref):
        self.filled(ref, name, ("sent", name[0])).wait_recv()

    def drain(self):
        for buffer, ref in self.sent.items():
            self.filled(ref, ("sent", buffer), ("sent", buffer)).wait_send()
        self.sent = {}


def reduce_kernel(
    g_ref, e_ref, table_ref, row_acc_ref, touched_ref,
    mean_ref, norm_ref, tab, emb, row_tab, row_sq, row_ra, flat_sq,
    acc, pair, idx, ra,
    a_relay, a_last, a_mid, a_end,
    b_relay, b_last, b_mid, b_end,
    c_far, c_chain, c_end,
    n_all,
    net_sems, load_sems,
):
    gx, gy = lax.axis_index("gx"), lax.axis_index("gy")
    x, z = gx // NZ, gx % NZ
    y, c = gy // NC, gy % NC

    def dev(dx=0, dy=0, dz=0, core=None):
        return (
            ((x + dx) % NX) * NZ + (z + dz) % NZ,
            ((y + dy) % NY) * NC + (c if core is None else core),
        )

    cols = lambda u: pl.ds(u * LANES, LANES)
    loads = {}
    for u in (0, 3, 6, 7, 1, 4, 2, 5):
        loads[u] = pltpu.make_async_copy(
            g_ref.at[:, :, :, c, :, cols(u)], acc.at[u], load_sems.at[u]
        )
        loads[u].start()
    prep_loads = [
        pltpu.make_async_copy(src, dst, load_sems.at[UNITS + i])
        for i, (src, dst) in enumerate(
            ((e_ref, emb), (touched_ref, idx), (row_acc_ref, ra), (table_ref, tab))
        )
    ]
    for copy in prep_loads:
        copy.start()

    barrier = pltpu.get_barrier_semaphore()
    nearby = [dev(core=1 - c)] + [dev(**{axis: step}) for axis in ("dx", "dy", "dz") for step in (1, -1)]
    for device in nearby:
        pl.semaphore_signal(barrier, inc=1, device_id=device, device_id_type=MESH)
    pl.semaphore_wait(barrier, len(nearby))

    other = 1 - c
    mate = dev(core=other)
    net = Net(net_sems, mate)
    kinds = {u: "x" if u < XS else "y" if u < XS + YS else "z" for u in range(UNITS)}

    def part(ref, u, k):
        if kinds[u] == "x":
            return ref.at[u, (x + k) % NX]
        if kinds[u] == "y":
            return ref.at[u, :, :, (y + k) % NY]
        return ref.at[u, :, (z + k) % NZ]

    def give(u, ks):
        for k in ks:
            if kinds[u] == "x":
                src = g_ref.at[(x + k) % NX, :, :, other, :, cols(u)]
            elif kinds[u] == "y":
                src = g_ref.at[:, :, (y + k) % NY, other, :, cols(u)]
            else:
                src = g_ref.at[:, (z + k) % NZ, :, other, :, cols(u)]
            net.start(("pair", u, ks), pair, src, part(pair, u, k), mate)

    loaded = set()

    def take(u, ks):
        if u not in loaded:
            loaded.add(u)
            loads[u].wait()
        if kinds[u] == "x":
            span = pair.at[u, pl.ds(0, len(ks))]
        elif kinds[u] == "y":
            span = pair.at[u, :, :, pl.ds(0, len(ks))]
        else:
            span = pair.at[u, :, pl.ds(0, len(ks))]
        net.wait(("pair", u, ks), span)
        for k in ks:
            mine = part(acc, u, k)
            mine[...] = mine[...] + part(pair, u, k)[...]

    FAR, NEAR, OWN = (2,), (1, 3), (0,)
    C1, C2, C3, C4 = (4,), (3, 5), (2, 6), (1, 7, 0)
    for us, ks in (
        ((0, 3), FAR), ((6, 7), C1), ((0, 3), NEAR), ((6, 7), C2), ((1, 4), FAR), ((6, 7), C3),
        ((1, 4), NEAR), ((2, 5), FAR), ((6, 7), C4), ((0, 3), OWN), ((2, 5), NEAR), ((1, 4, 2, 5), OWN),
    ):
        for u in us:
            give(u, ks)

    LO, HI = pl.ds(0, 4), pl.ds(4, 4)

    def tree(tag, axis, relay, last, view, mine):
        def far(w):
            net.start((tag + "r", w, 0), relay, view(w, 2, LO), relay.at[w, 0], dev(**{axis: 1}))
            net.start((tag + "r", w, 1), relay, view(w, 2, HI), relay.at[w, 1], dev(**{axis: -1}))

        def land(w, side, half):
            return last.at[w, side, half] if axis == "dx" else last.at[w, side, :, half]

        def near(w):
            net.start((tag + "l", w), last, view(w, 1, HI), land(w, 0, HI), dev(**{axis: 1}))
            net.start((tag + "l", w), last, view(w, 3, LO), land(w, 1, LO), dev(**{axis: -1}))

        def late(w):
            for side, k, half in ((0, 1, LO), (1, 3, HI)):
                net.wait((tag + "r", w, side), relay.at[w, side])
                ref = view(w, k, half)
                ref[...] = ref[...] + relay[w, side]
                net.start((tag + "l", w), last, ref, land(w, side, half), dev(**{axis: 1 - 2 * side}))

        def final(w):
            net.wait((tag + "l", w), last.at[w])
            ref = mine(w)
            ref[...] = ref[...] + (last[w, 0] + last[w, 1])

        return far, near, late, final

    a_steps = tree(
        "a", "dx", a_relay, a_last,
        lambda w, k, half: acc.at[w, (x + k) % NX, half],
        lambda w: acc.at[w, x],
    )

    def a_far(w):
        take(w, FAR)
        a_steps[0](w)

    def a_near(w):
        take(w, NEAR)
        a_steps[1](w)

    def a_late(w):
        a_steps[2](w)

    def a_two(w):
        take(w, OWN)
        a_steps[3](w)
        for k in (2, 1, 3):
            net.start(("am", w), a_mid, acc.at[w, x, :, (y + k) % NY], a_mid.at[w, k - 1], dev(dy=k))

    def line(tag, w, u, mid, ends):
        net.wait((tag + "m", w), mid.at[w])
        ref = acc.at[u, x, :, y]
        ref[...] = ref[...] + (mid[w, 0] + mid[w, 1] + mid[w, 2])
        for k in (4, 3, 5, 2, 6, 1, 7):
            net.start((tag + "e", w), ends, acc.at[u, x, (z + k) % NZ, y], ends.at[w, k - 1], dev(dz=k))

    def a_three(w):
        line("a", w, w, a_mid, a_end)

    b_steps = tree(
        "b", "dy", b_relay, b_last,
        lambda w, k, half: acc.at[XS + w, :, half, (y + k) % NY],
        lambda w: acc.at[XS + w, :, :, y],
    )

    def b_far(w):
        take(XS + w, FAR)
        b_steps[0](w)

    def b_near(w):
        take(XS + w, NEAR)
        b_steps[1](w)

    def b_late(w):
        b_steps[2](w)

    def b_two(w):
        take(XS + w, OWN)
        b_steps[3](w)
        for k in (2, 1, 3):
            net.start(("bm", w), b_mid, acc.at[XS + w, (x + k) % NX, :, y], b_mid.at[w, k - 1], dev(dx=k))

    def b_three(w):
        line("b", w, XS + w, b_mid, b_end)

    XLO, XHI = pl.ds(0, 2), pl.ds(2, 2)

    def c_part(w, k, half=slice(None)):
        return acc.at[XS + YS + w, half, (z + k) % NZ]

    def c_zero(w):
        take(XS + YS + w, C1)
        net.start(("cf", w, 0), c_far, c_part(w, 4, XLO), c_far.at[w, 0], dev(dz=1))
        net.start(("cf", w, 1), c_far, c_part(w, 4, XHI), c_far.at[w, 1], dev(dz=-1))

    def c_near(w):
        take(XS + YS + w, C2)
        net.start(("cc", w, 0, 0), c_chain, c_part(w, 3, XHI), c_chain.at[w, 0, 0, XHI], dev(dz=1))
        net.start(("cc", w, 1, 0), c_chain, c_part(w, 5, XLO), c_chain.at[w, 1, 0, XLO], dev(dz=-1))

    def c_one(w):
        for side, k, half in ((0, 3, XLO), (1, 5, XHI)):
            net.wait(("cf", w, side), c_far.at[w, side])
            ref = c_part(w, k, half)
            ref[...] = ref[...] + c_far[w, side]
            net.start(("cc", w, side, 0), c_chain, ref, c_chain.at[w, side, 0, half], dev(dz=1 - 2 * side))

    def c_pass(w, step, ks):
        for side, k in enumerate(ks):
            net.wait(("cc", w, side, step), c_chain.at[w, side, step])
            ref = c_part(w, k)
            ref[...] = ref[...] + c_chain[w, side, step]
            net.start(
                ("cc", w, side, step + 1), c_chain, ref, c_chain.at[w, side, step + 1], dev(dz=1 - 2 * side)
            )

    def c_two(w):
        take(XS + YS + w, C3)
        c_pass(w, 0, (2, 6))

    def c_three(w):
        take(XS + YS + w, C4)
        c_pass(w, 1, (1, 7))

    def c_four(w):
        for side in (0, 1):
            net.wait(("cc", w, side, 2), c_chain.at[w, side, 2])
        ref = c_part(w, 0)
        ref[...] = ref[...] + (c_chain[w, 0, 2] + c_chain[w, 1, 2])
        for dx, dy in PLANE:
            net.start(
                ("ce", w), c_end,
                acc.at[XS + YS + w, (x + dx) % NX, z, (y + dy) % NY],
                c_end.at[w, dx * NY + dy - 1],
                dev(dx=dx, dy=dy),
            )

    squares = []

    def prep_start():
        for copy in prep_loads:
            copy.wait()
        grads = emb[...]
        own = grads * grads
        squares.append(jnp.sum(own.reshape(-1, 8, LANES), axis=0))
        mean = jnp.sum(own, axis=1, keepdims=True) / F32(LANES)
        row_sq[...] = jnp.broadcast_to(mean, row_sq.shape)

    spot = lax.broadcasted_iota(jnp.int32, (32, LANES), 0) * LANES
    spot = spot + lax.broadcasted_iota(jnp.int32, (32, LANES), 1)
    flat = [jnp.zeros((32, LANES), F32)]

    def prep(part, parts=8):
        size = 512 // parts

        def eight(i, total):
            base = part * size + i * 8
            for j in range(8):
                t = base + j
                r = idx[t]
                row_tab[pl.ds(t, 1), :] = tab[pl.ds(r, 1), :]
                row_ra[pl.ds(t, 1), :] = jnp.full((1, LANES), ra[r], F32)
                total = jnp.where(spot == r, row_sq[pl.ds(t, 1), :], total)
            return total

        flat[0] = lax.fori_loop(0, size // 8, eight, flat[0])

    def end(u, name, w, ends):
        net.wait((name, w), ends.at[w])
        mean = (acc[u, x, z, y] + jnp.sum(ends[w], axis=0)) / F32(SHARDS)
        mean_ref[:, cols(u)] = mean
        squares.append(mean * mean)

    def a_end_step(w):
        end(w, "ae", w, a_end)

    def b_end_step(w):
        end(XS + w, "be", w, b_end)

    def c_end_step(w):
        end(XS + YS + w, "ce", w, c_end)

    a_far(0); b_far(0); c_zero(0); c_zero(1)
    a_near(0); b_near(0); c_near(0); c_near(1)
    a_far(1); b_far(1)
    c_one(0); a_late(0); b_late(0); c_one(1)
    a_near(1); b_near(1)
    a_far(2); b_far(2)
    prep_start()
    c_two(0)
    a_late(1); b_late(1)
    c_two(1)
    a_near(2); b_near(2)
    prep(0)
    prep(1)
    c_three(0); c_three(1)
    prep(2)
    a_late(2); b_late(2)
    a_two(0); b_two(0)
    prep(3)
    a_two(1); b_two(1)
    prep(4)
    a_two(2); b_two(2)
    c_four(0); c_four(1)
    prep(5)
    prep(6)
    a_three(0); b_three(0)
    a_three(1); b_three(1)
    prep(7)
    flat_sq[...] = flat[0]
    a_three(2); b_three(2)
    c_end_step(0)
    c_end_step(1)
    a_end_step(0); b_end_step(0)
    a_end_step(1); b_end_step(1)
    a_end_step(2); b_end_step(2)

    total = functools.reduce(lambda p, q: p + q, squares)
    n_all[pl.ds(0, 1), :] = jnp.sum(total, axis=0, keepdims=True)
    me = gx * (NY * NC) + gy
    own = n_all.at[pl.ds(0, 1)]
    rest = n_all.at[pl.ds(1, SHARDS - 1)]
    for k in RANKS:
        q = (me + k) % SHARDS
        device = (q // (NY * NC), q % (NY * NC))
        net.start(("norm",), rest, own, n_all.at[pl.ds(k, 1)], device)
    net.wait(("norm",), rest)
    norm_ref[...] = jnp.sum(n_all[...], axis=0, keepdims=True)
    net.drain()
    assert len(net.slots) == SEMS, len(net.slots)


def reduce_mean(grads, emb, table, row_acc, touched):
    vm = lambda *shape: pltpu.VMEM(shape + (8, LANES), F32)
    shapes = ((8, 1024), (1, LANES), table.shape) + (emb.shape,) * 4 + ((32, LANES),)
    return pl.pallas_call(
        reduce_kernel,
        name="reduce_mean",
        out_shape=[jax.ShapeDtypeStruct(shape, F32) for shape in shapes],
        in_specs=[pl.BlockSpec(memory_space=pltpu.HBM)] * 5,
        out_specs=[pl.BlockSpec(memory_space=pltpu.VMEM)] * len(shapes),
        scratch_shapes=[
            vm(UNITS, NX, NZ, NY),
            vm(UNITS, NX, NZ, NY),
            pltpu.SMEM(touched.shape, jnp.int32),
            pltpu.SMEM(row_acc.shape, F32),
            vm(XS, 2, 4, NY), vm(XS, 2, NZ, NY), vm(XS, 3, NZ), vm(XS, 7),
            vm(YS, 2, NX, 4), vm(YS, 2, NX, NZ), vm(YS, 3, NZ), vm(YS, 7),
            vm(ZS, 2, 2, NY), vm(ZS, 2, 3, NX, NY), vm(ZS, NX * NY - 1),
            pltpu.VMEM((SHARDS, LANES), F32),
            pltpu.SemaphoreType.DMA((SEMS,)),
            pltpu.SemaphoreType.DMA((UNITS + 4,)),
        ],
        compiler_params=pltpu.CompilerParams(
            collective_id=0, has_side_effects=True, vmem_limit_bytes=32 * 1024 * 1024
        ),
    )(*(
        pltpu.with_memory_space_constraint(value, pltpu.HBM)
        for value in (grads.reshape(NX, NZ, NY, NC, 8, 1024), emb, table, row_acc, touched)
    ))


def update_kernel(
    norm_ref, mean_ref, tab_ref, emb_ref, row_tab, row_sq, row_ra, flat_sq,
    param_ref, acc_ref, ra_ref, touched_ref,
    dense_out, dense_acc_out, table_out, row_acc_out, tab,
    idx, rows, dense_new, dense_acc_new, ra_new, sems,
):
    load = pltpu.make_async_copy(touched_ref, idx, sems.at[0])
    load.start()
    norm_sq = jnp.sum(norm_ref[...], axis=1, keepdims=True)
    clip = jnp.minimum(F32(1.0), F32(max_norm) / (jnp.sqrt(norm_sq) + F32(1e-06)))
    square = clip * clip
    live = clip > 0.0

    def grown(old, mean_square):
        return old + jnp.where(live, square * mean_square, 0.0)

    new_ra = grown(row_ra[...], row_sq[...])
    step = (F32(learn_rate) * clip) * emb_ref[...] / (jnp.sqrt(new_ra) + F32(epsilon))
    rows[...] = row_tab[...] - step
    load.wait()

    def sixteen(i, carry):
        for j in range(16):
            t = i * 16 + j
            tab[pl.ds(idx[t], 1), :] = rows[pl.ds(t, 1), :]
        return carry

    lax.fori_loop(0, 32, sixteen, 0)
    out = [pltpu.make_async_copy(tab, table_out, sems.at[1])]
    out[0].start()
    ra_new[...] = grown(ra_ref[...], flat_sq[...])
    scaled = clip * mean_ref[...]
    grow = acc_ref[...] + scaled * scaled
    dense_acc_new[...] = grow
    dense_new[...] = param_ref[...] - F32(learn_rate) * scaled / (jnp.sqrt(grow) + F32(epsilon))
    for i, (src, dst) in enumerate(
        ((ra_new, row_acc_out), (dense_acc_new, dense_acc_out), (dense_new, dense_out))
    ):
        out.append(pltpu.make_async_copy(src, dst, sems.at[2 + i]))
        out[-1].start()
    for copy in out:
        copy.wait()


def body(dense_grads, dense_param, dense_acc, table, row_acc, touched, emb_grads):
    mean, norm, tab, emb, row_tab, row_sq, row_ra, flat_sq = reduce_mean(
        dense_grads, emb_grads, table, row_acc, touched
    )
    vmem, hbm = pl.BlockSpec(memory_space=pltpu.VMEM), pl.BlockSpec(memory_space=pltpu.HBM)
    shapes = (dense_param.shape, dense_param.shape, table.shape, (32, LANES), table.shape)
    new_dense, new_dense_acc, new_table, new_row_acc, _ = pl.pallas_call(
        update_kernel,
        name="update",
        out_shape=[jax.ShapeDtypeStruct(shape, F32) for shape in shapes],
        in_specs=[vmem] * 11 + [hbm],
        out_specs=[hbm] * 4 + [vmem],
        scratch_shapes=[
            pltpu.SMEM(touched.shape, jnp.int32),
            pltpu.VMEM(emb.shape, F32),
            pltpu.VMEM(dense_param.shape, F32),
            pltpu.VMEM(dense_param.shape, F32),
            pltpu.VMEM((32, LANES), F32),
            pltpu.SemaphoreType.DMA((5,)),
        ],
        input_output_aliases={2: 4},
        compiler_params=pltpu.CompilerParams(vmem_limit_bytes=16 * 1024 * 1024),
    )(
        norm, mean, tab, emb, row_tab, row_sq, row_ra, flat_sq,
        dense_param, dense_acc, row_acc.reshape(32, LANES), touched,
    )
    return (new_dense, new_dense_acc, new_table, new_row_acc.reshape(-1))


def solution(mesh):
    return jax.shard_map(
        body,
        mesh=mesh,
        in_specs=(
            P(("gx", "gy"), None, None),
            P(("gx", "gy"), None),
            P(("gx", "gy"), None),
            P(("gx", "gy"), None),
            P(("gx", "gy")),
            P(("gx", "gy")),
            P(("gx", "gy"), None),
        ),
        out_specs=(
            P(("gx", "gy"), None),
            P(("gx", "gy"), None),
            P(("gx", "gy"), None),
            P(("gx", "gy")),
        ),
        check_vma=False,
    )
```

time: 322 us -> 49.1 us (0.15)
  waiting for transfers between devices: 201 us -> 0 us
  blocking collectives: 81.4 us -> 0 us
  Pallas kernels: 0 us -> 48.3 us
  other arithmetic: 15.3 us -> 0 us
  between operations: 15.5 us -> 0.7 us
  local copies, waits for them, and re-layouts: 7.25 us -> 0.02 us
    psum x1 -> x0, waiting for transfers between devices: 201 us -> none  [body(): summed, embed_total = lax.psum((local_grad, embed_square), ('gx', 'gy'))]
    psum x1 -> x0, blocking collectives: 81.4 us -> none  [body(): summed, embed_total = lax.psum((local_grad, embed_square), ('gx', 'gy'))]
    pallas_call x0 -> x2, Pallas kernels: none -> 48.3 us  [the longest x1 45.8 us: reduce_mean(): pl.pallas_call(reduce_kernel, name='reduce_mean', out_shape=[jax.ShapeDty...]
    reduce_sum x3 -> x0, other arithmetic: 10.2 us -> none  [the longest x1 9.38 us: body(): norm_sq = jnp.sum(mean_whole * mean_whole) + embed_total]
    scatter x1 -> x0, other arithmetic: 3.6 us -> none  [body(): new_table = table.at[touched].set(updated_rows)]
  transfers between devices with their start and end apart: 1 -> 0, of which waited for: 1 -> 0; matrix products, arithmetic and copies ran while one was open for 1% -> 0% of each run, Pallas kernels for 0% -> 0%
where the time goes in v3:
time: 49.1 us; the launch traced here: 49 us
  Pallas kernels  48.3 us (98%)
  between operations  0.7 us (1%)
    pallas_call x1, Pallas kernels, reduce_mean(): pl.pallas_call(reduce_kernel, name='reduce_mean', out_shape=[jax.ShapeDty...  45.8 us
    pallas_call x1, Pallas kernels, body(): pl.pallas_call(update_kernel, name='update', out_shape=[jax.ShapeDtypeStr...  2.5 us

profile of v3, /device:TPU:1, one launch (start us, length us, event | category | flops | bytes accessed | tf_op | source)
XLA Modules:
  0.0 49.0 jit_solution(17551877403776119395)
XLA Ops:
  0.6 0.0 copy-start
  0.6 0.0 copy-start.1
  0.7 0.0 copy-start.2
  0.7 0.0 copy-start.3
  0.7 45.8 %reduce_mean.1 = (f32[8,1024]{1,0:T(8,128)S(1)}, f32[1,128]{1,0:T(1,128)S(1)}, f32[4096,128]{1,0:T(8,128)S(1)}, f32[512,128]{1,0:T(8,128)S(1)}, f32[512,128]{1,0...) custom-call(f32[4,8,4,2,8,1024]{5,4,3,2,1,0:T(8,128)} %bitcast.4, ...), custom_call_target="tpu_custom_call" | custom-call | tf_op jit(solution)/shard_map/reduce_mean/pallas_call | solution.py:403
  46.5 0.0 copy-done
  46.5 0.0 copy-done.1
  46.5 0.0 copy-done.2
  46.5 0.0 copy-done.3
  46.5 2.5 %update.1 = (f32[8,1024]{1,0:T(8,128)}, f32[8,1024]{1,0:T(8,128)}, f32[4096,128]{1,0:T(8,128)}, f32[32,128]{1,0:T(8,128)}, f32[4096,128]{1,0:T(8,128)S(1)}) custom-call(f32[1,128]{1,0:T(1,128)S(1)} %get-tuple-element.16.norm_ref, f32[8,1024]{1,0:T(8,128)S(1)} %get-tuple-element.17.mean_ref, ...), custom_call_target="tpu_custom_call", output_to_operand_aliasing={{4}: (2, {})} | custom-call | tf_op jit(solution)/shard_map/update/pallas_call | solution.py:480
Async XLA Ops:
  0.6 45.8 %copy-start = (f32[4096]{0:T(1024)S(1)}, f32[4096]{0:T(1024)}, u32[]{:S(2)}) copy-start(f32[4096]{0:T(1024)} %row_acc_ref.1) | copy-start | bytes 49156
  0.6 45.8 %copy-start.1 = (f32[8,1024]{1,0:T(8,128)S(1)}, f32[8,1024]{1,0:T(8,128)}, u32[]{:S(2)}) copy-start(f32[8,1024]{1,0:T(8,128)} %param_ref.1) | copy-start | bytes 98308
  0.7 45.8 %copy-start.2 = (f32[8,1024]{1,0:T(8,128)S(1)}, f32[8,1024]{1,0:T(8,128)}, u32[]{:S(2)}) copy-start(f32[8,1024]{1,0:T(8,128)} %acc_ref.1) | copy-start | bytes 98308
  0.7 45.8 %copy-start.3 = (s32[512]{0:T(512)S(1)}, s32[512]{0:T(512)}, u32[]{:S(2)}) copy-start(s32[512]{0:T(512)} %touched_ref.3) | copy-start | bytes 6148

commit v4 on v3

--- a/solution.py
+++ b/solution.py
@@ -11,7 +11,7 @@
 max_norm = 8.0
 epsilon = 1e-10
 
-MESH = pl.DeviceIdType.MESH
+LOGICAL = pl.DeviceIdType.LOGICAL
 NX, NZ, NY, NC = 4, 8, 4, 2
 SHARDS = 256
 XS, YS, ZS = 3, 3, 2
@@ -27,12 +27,18 @@
 )
 
 
-def far(k):
-    dx, dz, dy = k // (NZ * NY * NC), k // (NY * NC) % NZ, k // NC % NY
-    return min(dx, NX - dx) + min(dz, NZ - dz) + min(dy, NY - dy)
-
-
-RANKS = sorted(range(1, SHARDS), key=lambda k: -far(k))
+def hops(dx, dy, dz):
+    return min(dx, NX - dx) + min(dy, NY - dy) + min(dz, NZ - dz)
+
+
+ALL = sorted(
+    [
+        (dx, dz, dy, dc)
+        for dx in range(NX) for dz in range(NZ) for dy in range(NY) for dc in range(NC)
+        if dx or dz or dy or dc
+    ],
+    key=lambda d: -hops(d[0], d[2], d[1]),
+)
 
 
 class Net:
@@ -51,7 +57,7 @@
             send_sem=self.sem(("sent", name[0])),
             recv_sem=self.sem(name),
             device_id=device,
-            device_id_type=MESH,
+            device_id_type=LOGICAL,
         ).start()
 
     def filled(self, ref, recv, sent):
@@ -61,7 +67,7 @@
             send_sem=self.sem(sent),
             recv_sem=self.sem(recv),
             device_id=self.mate,
-            device_id_type=MESH,
+            device_id_type=LOGICAL,
         )
 
     def wait(self, name, ref):
@@ -84,14 +90,18 @@
     net_sems, load_sems,
 ):
     gx, gy = lax.axis_index("gx"), lax.axis_index("gy")
-    x, z = gx // NZ, gx % NZ
-    y, c = gy // NC, gy % NC
-
-    def dev(dx=0, dy=0, dz=0, core=None):
-        return (
-            ((x + dx) % NX) * NZ + (z + dz) % NZ,
-            ((y + dy) % NY) * NC + (c if core is None else core),
-        )
+    x, z = lax.div(gx, NZ), lax.rem(gx, NZ)
+    y, c = lax.div(gy, NC), lax.rem(gy, NC)
+    at_x = [x] + [lax.rem(x + d, NX) for d in range(1, NX)]
+    at_y = [y] + [lax.rem(y + d, NY) for d in range(1, NY)]
+    at_z = [z] + [lax.rem(z + d, NZ) for d in range(1, NZ)]
+    at_c = [c, 1 - c]
+    base_x = [v * (NZ * NY * NC) for v in at_x]
+    base_z = [v * (NY * NC) for v in at_z]
+    base_y = [v * NC for v in at_y]
+
+    def dev(dx=0, dy=0, dz=0, dc=0):
+        return base_x[dx % NX] + base_z[dz % NZ] + (base_y[dy % NY] + at_c[dc])
 
     cols = lambda u: pl.ds(u * LANES, LANES)
     loads = {}
@@ -110,31 +120,31 @@
         copy.start()
 
     barrier = pltpu.get_barrier_semaphore()
-    nearby = [dev(core=1 - c)] + [dev(**{axis: step}) for axis in ("dx", "dy", "dz") for step in (1, -1)]
+    nearby = [dev(dc=1)] + [dev(**{axis: step}) for axis in ("dx", "dy", "dz") for step in (1, -1)]
     for device in nearby:
-        pl.semaphore_signal(barrier, inc=1, device_id=device, device_id_type=MESH)
+        pl.semaphore_signal(barrier, inc=1, device_id=device, device_id_type=LOGICAL)
     pl.semaphore_wait(barrier, len(nearby))
 
-    other = 1 - c
-    mate = dev(core=other)
+    other = at_c[1]
+    mate = dev(dc=1)
     net = Net(net_sems, mate)
     kinds = {u: "x" if u < XS else "y" if u < XS + YS else "z" for u in range(UNITS)}
 
     def part(ref, u, k):
         if kinds[u] == "x":
-            return ref.at[u, (x + k) % NX]
+            return ref.at[u, at_x[k]]
         if kinds[u] == "y":
-            return ref.at[u, :, :, (y + k) % NY]
-        return ref.at[u, :, (z + k) % NZ]
+            return ref.at[u, :, :, at_y[k]]
+        return ref.at[u, :, at_z[k]]
 
     def give(u, ks):
         for k in ks:
             if kinds[u] == "x":
-                src = g_ref.at[(x + k) % NX, :, :, other, :, cols(u)]
+                src = g_ref.at[at_x[k], :, :, other, :, cols(u)]
             elif kinds[u] == "y":
-                src = g_ref.at[:, :, (y + k) % NY, other, :, cols(u)]
+                src = g_ref.at[:, :, at_y[k], other, :, cols(u)]
             else:
-                src = g_ref.at[:, (z + k) % NZ, :, other, :, cols(u)]
+                src = g_ref.at[:, at_z[k], :, other, :, cols(u)]
             net.start(("pair", u, ks), pair, src, part(pair, u, k), mate)
 
     loaded = set()
@@ -193,7 +203,7 @@
 
     a_steps = tree(
         "a", "dx", a_relay, a_last,
-        lambda w, k, half: acc.at[w, (x + k) % NX, half],
+        lambda w, k, half: acc.at[w, at_x[k], half],
         lambda w: acc.at[w, x],
     )
 
@@ -212,21 +222,21 @@
         take(w, OWN)
         a_steps[3](w)
         for k in (2, 1, 3):
-            net.start(("am", w), a_mid, acc.at[w, x, :, (y + k) % NY], a_mid.at[w, k - 1], dev(dy=k))
+            net.start(("am", w), a_mid, acc.at[w, x, :, at_y[k]], a_mid.at[w, k - 1], dev(dy=k))
 
     def line(tag, w, u, mid, ends):
         net.wait((tag + "m", w), mid.at[w])
         ref = acc.at[u, x, :, y]
         ref[...] = ref[...] + (mid[w, 0] + mid[w, 1] + mid[w, 2])
         for k in (4, 3, 5, 2, 6, 1, 7):
-            net.start((tag + "e", w), ends, acc.at[u, x, (z + k) % NZ, y], ends.at[w, k - 1], dev(dz=k))
+            net.start((tag + "e", w), ends, acc.at[u, x, at_z[k], y], ends.at[w, k - 1], dev(dz=k))
 
     def a_three(w):
         line("a", w, w, a_mid, a_end)
 
     b_steps = tree(
         "b", "dy", b_relay, b_last,
-        lambda w, k, half: acc.at[XS + w, :, half, (y + k) % NY],
+        lambda w, k, half: acc.at[XS + w, :, half, at_y[k]],
         lambda w: acc.at[XS + w, :, :, y],
     )
 
@@ -245,7 +255,7 @@
         take(XS + w, OWN)
         b_steps[3](w)
         for k in (2, 1, 3):
-            net.start(("bm", w), b_mid, acc.at[XS + w, (x + k) % NX, :, y], b_mid.at[w, k - 1], dev(dx=k))
+            net.start(("bm", w), b_mid, acc.at[XS + w, at_x[k], :, y], b_mid.at[w, k - 1], dev(dx=k))
 
     def b_three(w):
         line("b", w, XS + w, b_mid, b_end)
@@ -253,7 +263,7 @@
     XLO, XHI = pl.ds(0, 2), pl.ds(2, 2)
 
     def c_part(w, k, half=slice(None)):
-        return acc.at[XS + YS + w, half, (z + k) % NZ]
+        return acc.at[XS + YS + w, half, at_z[k]]
 
     def c_zero(w):
         take(XS + YS + w, C1)
@@ -297,7 +307,7 @@
         for dx, dy in PLANE:
             net.start(
                 ("ce", w), c_end,
-                acc.at[XS + YS + w, (x + dx) % NX, z, (y + dy) % NY],
+                acc.at[XS + YS + w, at_x[dx], z, at_y[dy]],
                 c_end.at[w, dx * NY + dy - 1],
                 dev(dx=dx, dy=dy),
             )
@@ -347,50 +357,76 @@
     def c_end_step(w):
         end(XS + YS + w, "ce", w, c_end)
 
-    a_far(0); b_far(0); c_zero(0); c_zero(1)
-    a_near(0); b_near(0); c_near(0); c_near(1)
-    a_far(1); b_far(1)
-    c_one(0); a_late(0); b_late(0); c_one(1)
-    a_near(1); b_near(1)
-    a_far(2); b_far(2)
+    a_far(0)
+    b_far(0)
+    c_zero(1)
+    a_near(0)
+    b_near(0)
+    c_zero(0)
+    c_near(0)
+    b_far(1)
+    a_far(1)
+    a_near(1)
+    c_near(1)
+    a_late(0)
+    c_one(1)
+    b_late(0)
+    a_far(2)
+    c_one(0)
+    b_far(2)
+    b_near(1)
+    b_late(1)
+    a_late(1)
+    c_two(1)
+    a_near(2)
+    b_near(2)
+    c_two(0)
+    b_late(2)
+    a_two(0)
+    a_late(2)
+    b_two(0)
+    a_two(1)
+    c_three(1)
+    b_two(1)
+    c_three(0)
+    a_two(2)
+    b_two(2)
+    a_three(0)
+    b_three(0)
+    b_three(1)
+    c_four(0)
+    c_four(1)
+    a_three(1)
+    a_three(2)
+    b_three(2)
     prep_start()
-    c_two(0)
-    a_late(1); b_late(1)
-    c_two(1)
-    a_near(2); b_near(2)
     prep(0)
     prep(1)
-    c_three(0); c_three(1)
     prep(2)
-    a_late(2); b_late(2)
-    a_two(0); b_two(0)
     prep(3)
-    a_two(1); b_two(1)
     prep(4)
-    a_two(2); b_two(2)
-    c_four(0); c_four(1)
     prep(5)
     prep(6)
-    a_three(0); b_three(0)
-    a_three(1); b_three(1)
     prep(7)
     flat_sq[...] = flat[0]
-    a_three(2); b_three(2)
     c_end_step(0)
+    b_end_step(1)
     c_end_step(1)
-    a_end_step(0); b_end_step(0)
-    a_end_step(1); b_end_step(1)
-    a_end_step(2); b_end_step(2)
+    b_end_step(0)
+    a_end_step(0)
+    a_end_step(1)
+    a_end_step(2)
+    b_end_step(2)
 
     total = functools.reduce(lambda p, q: p + q, squares)
     n_all[pl.ds(0, 1), :] = jnp.sum(total, axis=0, keepdims=True)
-    me = gx * (NY * NC) + gy
     own = n_all.at[pl.ds(0, 1)]
     rest = n_all.at[pl.ds(1, SHARDS - 1)]
-    for k in RANKS:
-        q = (me + k) % SHARDS
-        device = (q // (NY * NC), q % (NY * NC))
-        net.start(("norm",), rest, own, n_all.at[pl.ds(k, 1)], device)
+    plane = [[base_x[dx] + base_z[dz] for dz in range(NZ)] for dx in range(NX)]
+    inner = [[base_y[dy] + at_c[dc] for dc in range(NC)] for dy in range(NY)]
+    for slot, (dx, dz, dy, dc) in enumerate(ALL, 1):
+        device = plane[dx][dz] + inner[dy][dc]
+        net.start(("norm",), rest, own, n_all.at[pl.ds(slot, 1)], device)
     net.wait(("norm",), rest)
     norm_ref[...] = jnp.sum(n_all[...], axis=0, keepdims=True)
     net.drain()

time: 49.1 us -> 46.9 us (0.955)
  Pallas kernels: 48.3 us -> 46.1 us
    pallas_call x1, Pallas kernels: 45.8 us -> 43.6 us  [reduce_mean(): pl.pallas_call(reduce_kernel, name='reduce_mean', out_shape=[jax.ShapeDty...]
where the time goes in v4:
time: 46.9 us; the launch traced here: 46.8 us
  Pallas kernels  46.1 us (98%)
  between operations  0.7 us (1%)
    pallas_call x1, Pallas kernels, reduce_mean(): pl.pallas_call(reduce_kernel, name='reduce_mean', out_shape=[jax.ShapeDty...  43.6 us
    pallas_call x1, Pallas kernels, body(): pl.pallas_call(update_kernel, name='update', out_shape=[jax.ShapeDtypeStr...  2.5 us

profile of v4, /device:TPU:1, one launch (start us, length us, event | category | flops | bytes accessed | tf_op | source)
XLA Modules:
  0.0 46.8 jit_solution(14839377845701520426)
XLA Ops:
  0.6 0.0 copy-start
  0.6 0.0 copy-start.1
  0.7 0.0 copy-start.2
  0.7 0.0 copy-start.3
  0.7 43.6 %reduce_mean.1 = (f32[8,1024]{1,0:T(8,128)S(1)}, f32[1,128]{1,0:T(1,128)S(1)}, f32[4096,128]{1,0:T(8,128)S(1)}, f32[512,128]{1,0:T(8,128)S(1)}, f32[512,128]{1,0...) custom-call(f32[4,8,4,2,8,1024]{5,4,3,2,1,0:T(8,128)} %bitcast.4, ...), custom_call_target="tpu_custom_call" | custom-call | tf_op jit(solution)/shard_map/reduce_mean/pallas_call | solution.py:439
  44.3 0.0 copy-done
  44.3 0.0 copy-done.1
  44.3 0.0 copy-done.2
  44.3 0.0 copy-done.3
  44.3 2.5 %update.1 = (f32[8,1024]{1,0:T(8,128)}, f32[8,1024]{1,0:T(8,128)}, f32[4096,128]{1,0:T(8,128)}, f32[32,128]{1,0:T(8,128)}, f32[4096,128]{1,0:T(8,128)S(1)}) custom-call(f32[1,128]{1,0:T(1,128)S(1)} %get-tuple-element.16.norm_ref, f32[8,1024]{1,0:T(8,128)S(1)} %get-tuple-element.17.mean_ref, ...), custom_call_target="tpu_custom_call", output_to_operand_aliasing={{4}: (2, {})} | custom-call | tf_op jit(solution)/shard_map/update/pallas_call | solution.py:516
Async XLA Ops:
  0.6 43.7 %copy-start = (f32[4096]{0:T(1024)S(1)}, f32[4096]{0:T(1024)}, u32[]{:S(2)}) copy-start(f32[4096]{0:T(1024)} %row_acc_ref.1) | copy-start | bytes 49156
  0.6 43.7 %copy-start.1 = (f32[8,1024]{1,0:T(8,128)S(1)}, f32[8,1024]{1,0:T(8,128)}, u32[]{:S(2)}) copy-start(f32[8,1024]{1,0:T(8,128)} %param_ref.1) | copy-start | bytes 98308
  0.7 43.7 %copy-start.2 = (f32[8,1024]{1,0:T(8,128)S(1)}, f32[8,1024]{1,0:T(8,128)}, u32[]{:S(2)}) copy-start(f32[8,1024]{1,0:T(8,128)} %acc_ref.1) | copy-start | bytes 98308
  0.7 43.7 %copy-start.3 = (s32[512]{0:T(512)S(1)}, s32[512]{0:T(512)}, u32[]{:S(2)}) copy-start(s32[512]{0:T(512)} %touched_ref.3) | copy-start | bytes 6148

commit v5 on v0

v5 whole, which is shorter than its diff:
```python
import functools

import jax
import jax.numpy as jnp
from jax import lax
from jax.experimental import pallas as pl
from jax.experimental.pallas import tpu as pltpu
from jax.sharding import PartitionSpec as P

learn_rate = 0.5
max_norm = 8.0
epsilon = 1e-10

LOGICAL = pl.DeviceIdType.LOGICAL
NX, NZ, NY, NC = 4, 8, 4, 2
SHARDS = 256
LANES = 128
F32 = jnp.float32

COLUMN = {"a0": 0, "a1": 1, "a2": 2, "b0": 3, "b1": 4, "b2": 5, "c0": 6, "c1": 7, "c2": (2, 5)}
WHOLE, MOST, REST = (8, LANES), (3, 2, LANES), (2, 2, LANES)
TILE = {u: WHOLE for u in COLUMN} | {"a2": MOST, "b2": MOST, "c2": REST}
WAVES = 3
SEMS, SENT_ROWS = 71, 16575

ORDER = (
    "b_far0", "a_far0", "c_zero0", "c_zero2", "b_far1", "b_far2", "a_near0", "a_far1", "c_zero1", "c_near0",
    "c_near2", "b_near1", "c_one0", "c_one2", "c_near1", "b_near0", "a_late0", "b_late0", "a_far2", "a_near1",
    "b_late1", "c_one1", "a_late1", "c_two0", "b_near2", "a_near2", "c_two2", "b_late2", "c_two1", "a_late2",
    "c_three0", "a_two0", "b_two1", "a_two1", "c_three2", "b_two0", "c_three1", "b_two2", "a_two2", "c_four0",
    "a_three0", "b_three1", "a_three1", "c_four2", "b_three0", "c_four1", "a_three2", "b_three2", "prep0",
    "prep1", "prep2", "prep3", "prep4", "prep5", "prep6", "prep7", "c_end0", "b_end0", "c_end2", "a_end0",
    "a_end1", "b_end1", "c_end1", "a_end2", "b_end2",
)

PLANE = sorted(
    [(dx, dy) for dx in range(NX) for dy in range(NY) if dx or dy],
    key=lambda d: -(min(d[0], NX - d[0]) + min(d[1], NY - d[1])),
)


def hops(dx, dy, dz):
    return min(dx, NX - dx) + min(dy, NY - dy) + min(dz, NZ - dz)


ALL = sorted(
    [
        (dx, dz, dy, dc)
        for dx in range(NX) for dz in range(NZ) for dy in range(NY) for dc in range(NC)
        if dx or dz or dy or dc
    ],
    key=lambda d: -hops(d[0], d[2], d[1]),
)


def size(ref):
    rows = 1
    for n in ref.shape[:-1]:
        rows *= n
    return rows


class Net:
    def __init__(self, sems, tally, mate):
        self.sems, self.tally, self.mate = sems, tally, mate
        self.slots, self.rows = {"sent": 0}, 0

    def sem(self, name):
        return self.sems.at[self.slots.setdefault(name, len(self.slots))]

    def start(self, name, src, dst, device):
        self.rows += size(src)
        pltpu.make_async_remote_copy(
            src_ref=src,
            dst_ref=dst,
            send_sem=self.sem("sent"),
            recv_sem=self.sem(name),
            device_id=device,
            device_id_type=LOGICAL,
        ).start()

    def filled(self, ref, name):
        return pltpu.make_async_remote_copy(
            src_ref=ref,
            dst_ref=ref,
            send_sem=self.sem("sent"),
            recv_sem=self.sem(name),
            device_id=self.mate,
            device_id_type=LOGICAL,
        )

    def wait(self, name, ref):
        self.filled(ref, name).wait_recv()

    def drain(self):
        self.filled(self.tally.at[pl.ds(0, self.rows)], "sent").wait_send()


def buffers(u):
    vm = lambda *shape: pltpu.VMEM(shape + TILE[u], F32)
    out = {"sum": vm(NX, NZ, NY), "pair": vm(NX, NZ, NY)}
    if u[0] == "a":
        out |= {"relay": vm(2, 4, NY), "last": vm(2, NZ, NY), "mid": vm(3, NZ), "end": vm(NZ - 1)}
    elif u[0] == "b":
        out |= {"relay": vm(2, NX, 4), "last": vm(2, NX, NZ), "mid": vm(3, NZ), "end": vm(NZ - 1)}
    else:
        out |= {"far": vm(2, 2, NY), "chain": vm(3, 2, NX, NY), "end": vm(NX * NY - 1)}
    return out


def reduce_kernel(
    g_ref, half_ref, e_ref, table_ref, row_acc_ref, touched_ref,
    mean_ref, norm_ref, tab, emb, row_tab, row_sq, row_ra, flat_sq,
    units, idx, ra, n_all, tally, net_sems, load_sems,
):
    gx, gy = lax.axis_index("gx"), lax.axis_index("gy")
    x, z = lax.div(gx, NZ), lax.rem(gx, NZ)
    y, c = lax.div(gy, NC), lax.rem(gy, NC)
    at_x = [x] + [lax.rem(x + d, NX) for d in range(1, NX)]
    at_y = [y] + [lax.rem(y + d, NY) for d in range(1, NY)]
    at_z = [z] + [lax.rem(z + d, NZ) for d in range(1, NZ)]
    at_c = [c, 1 - c]
    base_x = [v * (NZ * NY * NC) for v in at_x]
    base_z = [v * (NY * NC) for v in at_z]
    base_y = [v * NC for v in at_y]

    def dev(dx=0, dy=0, dz=0, dc=0):
        return base_x[dx % NX] + base_z[dz % NZ] + (base_y[dy % NY] + at_c[dc])

    every = slice(None)

    def rows_of(u, buffer, spot, core):
        if TILE[u] == WHOLE:
            return [(g_ref.at[(*spot, core, COLUMN[u])], buffer.at[spot])]
        if TILE[u] == MOST:
            return [(half_ref.at[(*spot, core, COLUMN[u], pl.ds(0, 3))], buffer.at[spot])]
        return [
            (half_ref.at[(*spot, core, column, 3)], buffer.at[(*spot, i)])
            for i, column in enumerate(COLUMN[u])
        ]

    loads, count = {}, 0
    for name in ORDER:
        u = name[0] + name[-1]
        if u in COLUMN and u not in loads:
            loads[u] = []
            for src, dst in rows_of(u, units[u]["sum"], (every, every, every), c):
                loads[u].append(pltpu.make_async_copy(src, dst, load_sems.at[count]))
                loads[u][-1].start()
                count += 1
    prep_loads = [
        pltpu.make_async_copy(src, dst, load_sems.at[count + i])
        for i, (src, dst) in enumerate(
            ((e_ref, emb), (touched_ref, idx), (row_acc_ref, ra), (table_ref, tab))
        )
    ]
    for copy in prep_loads:
        copy.start()

    barrier = pltpu.get_barrier_semaphore()
    nearby = [dev(dc=1)] + [dev(**{axis: step}) for axis in ("dx", "dy", "dz") for step in (1, -1)]
    for device in nearby:
        pl.semaphore_signal(barrier, inc=1, device_id=device, device_id_type=LOGICAL)
    pl.semaphore_wait(barrier, len(nearby))

    mate = dev(dc=1)
    net = Net(net_sems, tally, mate)

    def spot(u, k):
        if u[0] == "a":
            return (at_x[k], every, every)
        if u[0] == "b":
            return (every, every, at_y[k])
        return (every, at_z[k], every)

    FAR, NEAR, OWN = (2,), (1, 3), (0,)
    NEEDS = {
        "a_far": FAR, "a_near": NEAR, "a_two": OWN, "b_far": FAR, "b_near": NEAR, "b_two": OWN,
        "c_zero": (4,), "c_near": (3, 5), "c_two": (2, 6), "c_three": (1, 7, 0),
    }
    for name in ORDER:
        u = name[0] + name[-1]
        for k in NEEDS.get(name[:-1], ()):
            for src, dst in rows_of(u, units[u]["pair"], spot(u, k), at_c[1]):
                net.start(("pair", name), src, dst, mate)

    def take(name):
        u, ks = name[0] + name[-1], NEEDS.get(name[:-1], ())
        if not ks:
            return
        for copy in loads.pop(u, ()):
            copy.wait()
        some = pl.ds(0, len(ks))
        span = {"a": (some,), "b": (every, every, some), "c": (every, some)}[u[0]]
        net.wait(("pair", name), units[u]["pair"].at[span])
        for k in ks:
            mine = units[u]["sum"].at[spot(u, k)]
            mine[...] = mine[...] + units[u]["pair"].at[spot(u, k)][...]

    LO, HI = pl.ds(0, 4), pl.ds(4, 4)

    def view(u, k, half):
        total = units[u]["sum"]
        return total.at[at_x[k], half] if u[0] == "a" else total.at[:, half, at_y[k]]

    def land(u, side, half):
        last = units[u]["last"]
        return last.at[side, half] if u[0] == "a" else last.at[side, :, half]

    def first_axis(u, step):
        return dev(dx=step) if u[0] == "a" else dev(dy=step)

    def far(u):
        for side, half in enumerate((LO, HI)):
            net.start(("relay", u), view(u, 2, half), units[u]["relay"].at[side], first_axis(u, 1 - 2 * side))

    def near(u):
        for side, k, half in ((0, 1, HI), (1, 3, LO)):
            net.start(("last", u), view(u, k, half), land(u, side, half), first_axis(u, 1 - 2 * side))

    def late(u):
        relay = units[u]["relay"]
        net.wait(("relay", u), relay)
        for side, k, half in ((0, 1, LO), (1, 3, HI)):
            ref = view(u, k, half)
            ref[...] = ref[...] + relay[side]
            net.start(("last", u), ref, land(u, side, half), first_axis(u, 1 - 2 * side))

    def two(u):
        last, total = units[u]["last"], units[u]["sum"]
        net.wait(("last", u), last)
        ref = total.at[spot(u, 0)]
        ref[...] = ref[...] + (last[0] + last[1])
        for k in (2, 1, 3):
            if u[0] == "a":
                src, device = total.at[x, :, at_y[k]], dev(dy=k)
            else:
                src, device = total.at[at_x[k], :, y], dev(dx=k)
            net.start(("mid", u), src, units[u]["mid"].at[k - 1], device)

    def three(u):
        mid, total = units[u]["mid"], units[u]["sum"]
        net.wait(("mid", u), mid)
        ref = total.at[x, :, y]
        ref[...] = ref[...] + (mid[0] + mid[1] + mid[2])
        for k in (4, 3, 5, 2, 6, 1, 7):
            net.start(("end", u), total.at[x, at_z[k], y], units[u]["end"].at[k - 1], dev(dz=k))

    XLO, XHI = pl.ds(0, 2), pl.ds(2, 2)

    def c_part(u, k, half=every):
        return units[u]["sum"].at[half, at_z[k]]

    def c_zero(u):
        for side, half in enumerate((XLO, XHI)):
            net.start(("far", u), c_part(u, 4, half), units[u]["far"].at[side], dev(dz=1 - 2 * side))

    def c_near(u):
        for side, k, half in ((0, 3, XHI), (1, 5, XLO)):
            net.start(("chain", u, 0), c_part(u, k, half), units[u]["chain"].at[0, side, half], dev(dz=1 - 2 * side))

    def c_one(u):
        net.wait(("far", u), units[u]["far"])
        for side, k, half in ((0, 3, XLO), (1, 5, XHI)):
            ref = c_part(u, k, half)
            ref[...] = ref[...] + units[u]["far"][side]
            net.start(("chain", u, 0), ref, units[u]["chain"].at[0, side, half], dev(dz=1 - 2 * side))

    def c_pass(u, step, ks):
        chain = units[u]["chain"]
        net.wait(("chain", u, step), chain.at[step])
        for side, k in enumerate(ks):
            ref = c_part(u, k)
            ref[...] = ref[...] + chain[step, side]
            net.start(("chain", u, step + 1), ref, chain.at[step + 1, side], dev(dz=1 - 2 * side))

    def c_four(u):
        chain = units[u]["chain"]
        net.wait(("chain", u, 2), chain.at[2])
        ref = c_part(u, 0)
        ref[...] = ref[...] + (chain[2, 0] + chain[2, 1])
        for dx, dy in PLANE:
            net.start(
                ("end", u), units[u]["sum"].at[at_x[dx], z, at_y[dy]],
                units[u]["end"].at[dx * NY + dy - 1], dev(dx=dx, dy=dy),
            )

    squares = []

    def end(u):
        ends = units[u]["end"]
        net.wait(("end", u), ends)
        mean = (units[u]["sum"][x, z, y] + jnp.sum(ends[...], axis=0)) / F32(SHARDS)
        cols = lambda column: pl.ds(column * LANES, LANES)
        if TILE[u] == WHOLE:
            mean_ref[:, cols(COLUMN[u])] = mean
            squares.append(jnp.sum(mean * mean, axis=0, keepdims=True))
            return
        for i in range(TILE[u][0]):
            row, column = (2 * i, COLUMN[u]) if TILE[u] == MOST else (6, COLUMN[u][i])
            mean_ref[pl.ds(row, 2), cols(column)] = mean[i]
            squares.append(jnp.sum(mean[i] * mean[i], axis=0, keepdims=True))

    def prep_start():
        for copy in prep_loads:
            copy.wait()
        grads = emb[...]
        own = grads * grads
        squares.append(jnp.sum(own, axis=0, keepdims=True))
        mean = jnp.sum(own, axis=1, keepdims=True) / F32(LANES)
        row_sq[...] = jnp.broadcast_to(mean, row_sq.shape)

    place = lax.broadcasted_iota(jnp.int32, (32, LANES), 0) * LANES
    place = place + lax.broadcasted_iota(jnp.int32, (32, LANES), 1)
    flat = [jnp.zeros((32, LANES), F32)]

    def prep(part, parts=8):
        size = 512 // parts
        if part == 0:
            prep_start()

        def eight(i, total):
            base = part * size + i * 8
            for j in range(8):
                t = base + j
                r = idx[t]
                row_tab[pl.ds(t, 1), :] = tab[pl.ds(r, 1), :]
                row_ra[pl.ds(t, 1), :] = jnp.full((1, LANES), ra[r], F32)
                total = jnp.where(place == r, row_sq[pl.ds(t, 1), :], total)
            return total

        flat[0] = lax.fori_loop(0, size // 8, eight, flat[0])
        if part == parts - 1:
            flat_sq[...] = flat[0]

    steps = {
        "a_far": far, "a_near": near, "a_late": late, "a_two": two, "a_three": three, "a_end": end,
        "b_far": far, "b_near": near, "b_late": late, "b_two": two, "b_three": three, "b_end": end,
        "c_zero": c_zero, "c_near": c_near, "c_one": c_one,
        "c_two": lambda u: c_pass(u, 0, (2, 6)), "c_three": lambda u: c_pass(u, 1, (1, 7)),
        "c_four": c_four, "c_end": end,
    }
    for name in ORDER:
        with jax.named_scope(name):
            if name[:4] == "prep":
                prep(int(name[4:]))
            else:
                take(name)
                steps[name[:-1]](name[0] + name[-1])

    n_all[pl.ds(0, 1), :] = functools.reduce(lambda p, q: p + q, squares)
    own = n_all.at[pl.ds(0, 1)]
    rest = n_all.at[pl.ds(1, SHARDS - 1)]
    plane = [[base_x[dx] + base_z[dz] for dz in range(NZ)] for dx in range(NX)]
    inner = [[base_y[dy] + at_c[dc] for dc in range(NC)] for dy in range(NY)]
    for slot, (dx, dz, dy, dc) in enumerate(ALL, 1):
        device = plane[dx][dz] + inner[dy][dc]
        net.start("norm", own, n_all.at[pl.ds(slot, 1)], device)
    with jax.named_scope("nwait"):
        net.wait("norm", rest)
    norm_ref[...] = jnp.sum(n_all[...], axis=0, keepdims=True)
    with jax.named_scope("drain"):
        net.drain()
    assert (len(net.slots), net.rows) == (SEMS, SENT_ROWS), (len(net.slots), net.rows)


def reduce_mean(grads, emb, table, row_acc, touched):
    shapes = ((8, 1024), (1, LANES), table.shape) + (emb.shape,) * 4 + ((32, LANES),)
    tiles = grads.reshape(SHARDS, 8, 8, LANES).transpose(0, 2, 1, 3)
    return pl.pallas_call(
        reduce_kernel,
        name="reduce_mean",
        out_shape=[jax.ShapeDtypeStruct(shape, F32) for shape in shapes],
        in_specs=[pl.BlockSpec(memory_space=pltpu.HBM)] * 6,
        out_specs=[pl.BlockSpec(memory_space=pltpu.VMEM)] * len(shapes),
        scratch_shapes=[
            {u: buffers(u) for u in COLUMN},
            pltpu.SMEM(touched.shape, jnp.int32),
            pltpu.SMEM(row_acc.shape, F32),
            pltpu.VMEM((SHARDS, LANES), F32),
            pltpu.VMEM((SENT_ROWS, LANES), F32),
            pltpu.SemaphoreType.DMA((SEMS,)),
            pltpu.SemaphoreType.DMA((len(COLUMN) + 1 + 4,)),
        ],
        compiler_params=pltpu.CompilerParams(
            collective_id=0, has_side_effects=True, vmem_limit_bytes=40 * 1024 * 1024
        ),
    )(*(
        pltpu.with_memory_space_constraint(value, pltpu.HBM)
        for value in (
            tiles.reshape(NX, NZ, NY, NC, 8, *WHOLE),
            tiles.reshape(NX, NZ, NY, NC, 8, 4, 2, LANES),
            emb, table, row_acc, touched,
        )
    ))


def update_kernel(
    norm_ref, mean_ref, tab_ref, emb_ref, row_tab, row_sq, row_ra, flat_sq,
    param_ref, acc_ref, ra_ref, touched_ref,
    dense_out, dense_acc_out, table_out, row_acc_out, tab,
    idx, rows, dense_new, dense_acc_new, ra_new, sems,
):
    load = pltpu.make_async_copy(touched_ref, idx, sems.at[0])
    load.start()
    norm_sq = jnp.sum(norm_ref[...], axis=1, keepdims=True)
    clip = jnp.minimum(F32(1.0), F32(max_norm) / (jnp.sqrt(norm_sq) + F32(1e-06)))
    square = clip * clip
    live = clip > 0.0

    def grown(old, mean_square):
        return old + jnp.where(live, square * mean_square, 0.0)

    new_ra = grown(row_ra[...], row_sq[...])
    step = (F32(learn_rate) * clip) * emb_ref[...] / (jnp.sqrt(new_ra) + F32(epsilon))
    rows[...] = row_tab[...] - step
    load.wait()

    def sixteen(i, carry):
        for j in range(16):
            t = i * 16 + j
            tab[pl.ds(idx[t], 1), :] = rows[pl.ds(t, 1), :]
        return carry

    lax.fori_loop(0, 32, sixteen, 0)
    out = [pltpu.make_async_copy(tab, table_out, sems.at[1])]
    out[0].start()
    ra_new[...] = grown(ra_ref[...], flat_sq[...])
    scaled = clip * mean_ref[...]
    grow = acc_ref[...] + scaled * scaled
    dense_acc_new[...] = grow
    dense_new[...] = param_ref[...] - F32(learn_rate) * scaled / (jnp.sqrt(grow) + F32(epsilon))
    for i, (src, dst) in enumerate(
        ((ra_new, row_acc_out), (dense_acc_new, dense_acc_out), (dense_new, dense_out))
    ):
        out.append(pltpu.make_async_copy(src, dst, sems.at[2 + i]))
        out[-1].start()
    for copy in out:
        copy.wait()


def body(dense_grads, dense_param, dense_acc, table, row_acc, touched, emb_grads):
    mean, norm, tab, emb, row_tab, row_sq, row_ra, flat_sq = reduce_mean(
        dense_grads, emb_grads, table, row_acc, touched
    )
    vmem, hbm = pl.BlockSpec(memory_space=pltpu.VMEM), pl.BlockSpec(memory_space=pltpu.HBM)
    shapes = (dense_param.shape, dense_param.shape, table.shape, (32, LANES), table.shape)
    new_dense, new_dense_acc, new_table, new_row_acc, _ = pl.pallas_call(
        update_kernel,
        name="update",
        out_shape=[jax.ShapeDtypeStruct(shape, F32) for shape in shapes],
        in_specs=[vmem] * 11 + [hbm],
        out_specs=[hbm] * 4 + [vmem],
        scratch_shapes=[
            pltpu.SMEM(touched.shape, jnp.int32),
            pltpu.VMEM(emb.shape, F32),
            pltpu.VMEM(dense_param.shape, F32),
            pltpu.VMEM(dense_param.shape, F32),
            pltpu.VMEM((32, LANES), F32),
            pltpu.SemaphoreType.DMA((5,)),
        ],
        input_output_aliases={2: 4},
        compiler_params=pltpu.CompilerParams(vmem_limit_bytes=16 * 1024 * 1024),
    )(
        norm, mean, tab, emb, row_tab, row_sq, row_ra, flat_sq,
        dense_param, dense_acc, row_acc.reshape(32, LANES), touched,
    )
    return (new_dense, new_dense_acc, new_table, new_row_acc.reshape(-1))


def solution(mesh):
    return jax.shard_map(
        body,
        mesh=mesh,
        in_specs=(
            P(("gx", "gy"), None, None),
            P(("gx", "gy"), None),
            P(("gx", "gy"), None),
            P(("gx", "gy"), None),
            P(("gx", "gy")),
            P(("gx", "gy")),
            P(("gx", "gy"), None),
        ),
        out_specs=(
            P(("gx", "gy"), None),
            P(("gx", "gy"), None),
            P(("gx", "gy"), None),
            P(("gx", "gy")),
        ),
        check_vma=False,
    )
```

time: 322 us -> 45.2 us (0.14)
  waiting for transfers between devices: 201 us -> 0 us
  blocking collectives: 81.4 us -> 0 us
  Pallas kernels: 0 us -> 44.4 us
  other arithmetic: 15.3 us -> 0 us
  between operations: 15.5 us -> 0.7 us
  local copies, waits for them, and re-layouts: 7.25 us -> 0.02 us
    psum x1 -> x0, waiting for transfers between devices: 201 us -> none  [body(): summed, embed_total = lax.psum((local_grad, embed_square), ('gx', 'gy'))]
    psum x1 -> x0, blocking collectives: 81.4 us -> none  [body(): summed, embed_total = lax.psum((local_grad, embed_square), ('gx', 'gy'))]
    pallas_call x0 -> x2, Pallas kernels: none -> 44.4 us  [the longest x1 41.9 us: reduce_mean(): pl.pallas_call(reduce_kernel, name='reduce_mean', out_shape=[jax.ShapeDty...]
    reduce_sum x3 -> x0, other arithmetic: 10.2 us -> none  [the longest x1 9.38 us: body(): norm_sq = jnp.sum(mean_whole * mean_whole) + embed_total]
    scatter x1 -> x0, other arithmetic: 3.6 us -> none  [body(): new_table = table.at[touched].set(updated_rows)]
  transfers between devices with their start and end apart: 1 -> 0, of which waited for: 1 -> 0; matrix products, arithmetic and copies ran while one was open for 1% -> 0% of each run, Pallas kernels for 0% -> 0%
where the time goes in v5:
time: 45.2 us; the launch traced here: 45.1 us
  Pallas kernels  44.4 us (98%)
  between operations  0.7 us (2%)
    pallas_call x1, Pallas kernels, reduce_mean(): pl.pallas_call(reduce_kernel, name='reduce_mean', out_shape=[jax.ShapeDty...  41.9 us
    pallas_call x1, Pallas kernels, body(): pl.pallas_call(update_kernel, name='update', out_shape=[jax.ShapeDtypeStr...  2.5 us

profile of v5, /device:TPU:1, one launch (start us, length us, event | category | flops | bytes accessed | tf_op | source)
XLA Modules:
  0.0 45.1 jit_solution(15923595086638285920)
XLA Ops:
  0.6 0.0 copy-start
  0.6 0.0 copy-start.1
  0.7 0.0 copy-start.2
  0.7 0.0 copy-start.3
  0.7 41.9 %reduce_mean.1 = (f32[8,1024]{1,0:T(8,128)S(1)}, f32[1,128]{1,0:T(1,128)S(1)}, f32[4096,128]{1,0:T(8,128)S(1)}, f32[512,128]{1,0:T(8,128)S(1)}, f32[512,128]{1,0...) custom-call(f32[4,8,4,2,8,8,128]{6,5,4,3,2,1,0:T(8,128)} %bitcast.10, ...), custom_call_target="tpu_custom_call" | custom-call | tf_op jit(solution)/shard_map/reduce_mean/pallas_call | solution.py:370
  42.5 0.0 copy-done
  42.5 0.0 copy-done.1
  42.6 0.0 copy-done.2
  42.6 0.0 copy-done.3
  42.6 2.5 %update.1 = (f32[8,1024]{1,0:T(8,128)}, f32[8,1024]{1,0:T(8,128)}, f32[4096,128]{1,0:T(8,128)}, f32[32,128]{1,0:T(8,128)}, f32[4096,128]{1,0:T(8,128)S(1)}) custom-call(f32[1,128]{1,0:T(1,128)S(1)} %get-tuple-element.16.norm_ref, f32[8,1024]{1,0:T(8,128)S(1)} %get-tuple-element.17.mean_ref, ...), custom_call_target="tpu_custom_call", output_to_operand_aliasing={{4}: (2, {})} | custom-call | tf_op jit(solution)/shard_map/update/pallas_call | solution.py:448
Async XLA Ops:
  0.6 41.9 %copy-start = (f32[4096]{0:T(1024)S(1)}, f32[4096]{0:T(1024)}, u32[]{:S(2)}) copy-start(f32[4096]{0:T(1024)} %row_acc_ref.1) | copy-start | bytes 49156
  0.6 41.9 %copy-start.1 = (f32[8,1024]{1,0:T(8,128)S(1)}, f32[8,1024]{1,0:T(8,128)}, u32[]{:S(2)}) copy-start(f32[8,1024]{1,0:T(8,128)} %param_ref.1) | copy-start | bytes 98308
  0.7 41.9 %copy-start.2 = (f32[8,1024]{1,0:T(8,128)S(1)}, f32[8,1024]{1,0:T(8,128)}, u32[]{:S(2)}) copy-start(f32[8,1024]{1,0:T(8,128)} %acc_ref.1) | copy-start | bytes 98308
  0.7 41.9 %copy-start.3 = (s32[512]{0:T(512)S(1)}, s32[512]{0:T(512)}, u32[]{:S(2)}) copy-start(s32[512]{0:T(512)} %touched_ref.3) | copy-start | bytes 6148

commit v6 on v5

--- a/solution.py
+++ b/solution.py
@@ -17,20 +17,23 @@
 LANES = 128
 F32 = jnp.float32
 
-COLUMN = {"a0": 0, "a1": 1, "a2": 2, "b0": 3, "b1": 4, "b2": 5, "c0": 6, "c1": 7, "c2": (2, 5)}
-WHOLE, MOST, REST = (8, LANES), (3, 2, LANES), (2, 2, LANES)
-TILE = {u: WHOLE for u in COLUMN} | {"a2": MOST, "b2": MOST, "c2": REST}
-WAVES = 3
-SEMS, SENT_ROWS = 71, 16575
+UNITS = {
+    "a0": (0, None), "a1": (1, None), "a2": (2, 0),
+    "b0": (3, None), "b1": (4, None), "b2": (5, 0),
+    "c0": (2, 1), "c1": (5, 1), "c2": (6, None), "c3": (7, None),
+}
+TILE = {u: (8, LANES) if rows is None else (4, LANES) for u, (_, rows) in UNITS.items()}
+SEMS, SENT_ROWS = 70, 16575
 
 ORDER = (
-    "b_far0", "a_far0", "c_zero0", "c_zero2", "b_far1", "b_far2", "a_near0", "a_far1", "c_zero1", "c_near0",
-    "c_near2", "b_near1", "c_one0", "c_one2", "c_near1", "b_near0", "a_late0", "b_late0", "a_far2", "a_near1",
-    "b_late1", "c_one1", "a_late1", "c_two0", "b_near2", "a_near2", "c_two2", "b_late2", "c_two1", "a_late2",
-    "c_three0", "a_two0", "b_two1", "a_two1", "c_three2", "b_two0", "c_three1", "b_two2", "a_two2", "c_four0",
-    "a_three0", "b_three1", "a_three1", "c_four2", "b_three0", "c_four1", "a_three2", "b_three2", "prep0",
-    "prep1", "prep2", "prep3", "prep4", "prep5", "prep6", "prep7", "c_end0", "b_end0", "c_end2", "a_end0",
-    "a_end1", "b_end1", "c_end1", "a_end2", "b_end2",
+    "c_zero1", "a_far2", "c_zero2", "b_far2", "c_near1", "b_far1", "c_zero0", "c_near0", "c_zero3", "a_near2",
+    "c_near2", "a_far0", "b_near2", "b_far0", "b_near0", "a_near0", "c_one1", "c_one2", "a_late2", "b_late2",
+    "c_one0", "c_near3", "b_near1", "a_far1", "c_one3", "b_late1", "a_late0", "c_two1", "c_two2", "c_two0",
+    "a_near1", "b_late0", "c_two3", "a_late1", "c_three1", "a_two2", "b_two2", "b_two1", "a_two0", "c_three2",
+    "c_three0", "b_two0", "c_three3", "a_two1", "a_three2", "b_three1", "b_three2", "c_four2", "a_three0",
+    "c_four0", "b_three0", "c_four1", "c_four3", "a_three1",
+    "c_end2", "c_end1", "b_end1", "a_end0", "b_end0", "a_end2", "b_end2", "c_end0",
+    "a_end1", "c_end3",
 )
 
 PLANE = sorted(
@@ -129,27 +132,27 @@
 
     every = slice(None)
 
-    def rows_of(u, buffer, spot, core):
-        if TILE[u] == WHOLE:
-            return [(g_ref.at[(*spot, core, COLUMN[u])], buffer.at[spot])]
-        if TILE[u] == MOST:
-            return [(half_ref.at[(*spot, core, COLUMN[u], pl.ds(0, 3))], buffer.at[spot])]
-        return [
-            (half_ref.at[(*spot, core, column, 3)], buffer.at[(*spot, i)])
-            for i, column in enumerate(COLUMN[u])
-        ]
-
-    loads, count = {}, 0
+    barrier = pltpu.get_barrier_semaphore()
+    nearby = [dev(dc=1)] + [dev(**{axis: step}) for axis in ("dx", "dy", "dz") for step in (1, -1)]
+    for device in nearby:
+        pl.semaphore_signal(barrier, inc=1, device_id=device, device_id_type=LOGICAL)
+
+    def rows_of(u, spot, core):
+        column, rows = UNITS[u]
+        if rows is None:
+            return g_ref.at[(*spot, core, column)]
+        return half_ref.at[(*spot, core, column, rows)]
+
+    loads = {}
     for name in ORDER:
         u = name[0] + name[-1]
-        if u in COLUMN and u not in loads:
-            loads[u] = []
-            for src, dst in rows_of(u, units[u]["sum"], (every, every, every), c):
-                loads[u].append(pltpu.make_async_copy(src, dst, load_sems.at[count]))
-                loads[u][-1].start()
-                count += 1
+        if u in UNITS and u not in loads:
+            loads[u] = pltpu.make_async_copy(
+                rows_of(u, (every, every, every), c), units[u]["sum"], load_sems.at[len(loads)]
+            )
+            loads[u].start()
     prep_loads = [
-        pltpu.make_async_copy(src, dst, load_sems.at[count + i])
+        pltpu.make_async_copy(src, dst, load_sems.at[len(UNITS) + i])
         for i, (src, dst) in enumerate(
             ((e_ref, emb), (touched_ref, idx), (row_acc_ref, ra), (table_ref, tab))
         )
@@ -157,10 +160,6 @@
     for copy in prep_loads:
         copy.start()
 
-    barrier = pltpu.get_barrier_semaphore()
-    nearby = [dev(dc=1)] + [dev(**{axis: step}) for axis in ("dx", "dy", "dz") for step in (1, -1)]
-    for device in nearby:
-        pl.semaphore_signal(barrier, inc=1, device_id=device, device_id_type=LOGICAL)
     pl.semaphore_wait(barrier, len(nearby))
 
     mate = dev(dc=1)
@@ -173,23 +172,23 @@
             return (every, every, at_y[k])
         return (every, at_z[k], every)
 
-    FAR, NEAR, OWN = (2,), (1, 3), (0,)
+    FAR, NEAR = (2,), (1, 3, 0)
     NEEDS = {
-        "a_far": FAR, "a_near": NEAR, "a_two": OWN, "b_far": FAR, "b_near": NEAR, "b_two": OWN,
-        "c_zero": (4,), "c_near": (3, 5), "c_two": (2, 6), "c_three": (1, 7, 0),
+        "a_far": FAR, "a_near": NEAR, "b_far": FAR, "b_near": NEAR,
+        "c_zero": (4,), "c_near": (3, 5), "c_two": (2, 6, 1, 7, 0),
     }
     for name in ORDER:
         u = name[0] + name[-1]
         for k in NEEDS.get(name[:-1], ()):
-            for src, dst in rows_of(u, units[u]["pair"], spot(u, k), at_c[1]):
-                net.start(("pair", name), src, dst, mate)
+            src = rows_of(u, spot(u, k), at_c[1])
+            net.start(("pair", name), src, units[u]["pair"].at[spot(u, k)], mate)
 
     def take(name):
         u, ks = name[0] + name[-1], NEEDS.get(name[:-1], ())
         if not ks:
             return
-        for copy in loads.pop(u, ()):
-            copy.wait()
+        if u in loads:
+            loads.pop(u).wait()
         some = pl.ds(0, len(ks))
         span = {"a": (some,), "b": (every, every, some), "c": (every, some)}[u[0]]
         net.wait(("pair", name), units[u]["pair"].at[span])
@@ -291,15 +290,10 @@
         ends = units[u]["end"]
         net.wait(("end", u), ends)
         mean = (units[u]["sum"][x, z, y] + jnp.sum(ends[...], axis=0)) / F32(SHARDS)
-        cols = lambda column: pl.ds(column * LANES, LANES)
-        if TILE[u] == WHOLE:
-            mean_ref[:, cols(COLUMN[u])] = mean
-            squares.append(jnp.sum(mean * mean, axis=0, keepdims=True))
-            return
-        for i in range(TILE[u][0]):
-            row, column = (2 * i, COLUMN[u]) if TILE[u] == MOST else (6, COLUMN[u][i])
-            mean_ref[pl.ds(row, 2), cols(column)] = mean[i]
-            squares.append(jnp.sum(mean[i] * mean[i], axis=0, keepdims=True))
+        column, rows = UNITS[u]
+        spot = slice(None) if rows is None else pl.ds(4 * rows, 4)
+        mean_ref[spot, pl.ds(column * LANES, LANES)] = mean
+        squares.append(jnp.sum(mean * mean, axis=0, keepdims=True))
 
     def prep_start():
         for copy in prep_loads:
@@ -316,9 +310,6 @@
 
     def prep(part, parts=8):
         size = 512 // parts
-        if part == 0:
-            prep_start()
-
         def eight(i, total):
             base = part * size + i * 8
             for j in range(8):
@@ -342,11 +333,10 @@
     }
     for name in ORDER:
         with jax.named_scope(name):
-            if name[:4] == "prep":
-                prep(int(name[4:]))
-            else:
-                take(name)
-                steps[name[:-1]](name[0] + name[-1])
+            take(name)
+            steps[name[:-1]](name[0] + name[-1])
+        if name == ORDER[-len(UNITS) - 1]:
+            prep_start()
 
     n_all[pl.ds(0, 1), :] = functools.reduce(lambda p, q: p + q, squares)
     own = n_all.at[pl.ds(0, 1)]
@@ -356,6 +346,8 @@
     for slot, (dx, dz, dy, dc) in enumerate(ALL, 1):
         device = plane[dx][dz] + inner[dy][dc]
         net.start("norm", own, n_all.at[pl.ds(slot, 1)], device)
+    for part in range(8):
+        prep(part)
     with jax.named_scope("nwait"):
         net.wait("norm", rest)
     norm_ref[...] = jnp.sum(n_all[...], axis=0, keepdims=True)
@@ -374,13 +366,13 @@
         in_specs=[pl.BlockSpec(memory_space=pltpu.HBM)] * 6,
         out_specs=[pl.BlockSpec(memory_space=pltpu.VMEM)] * len(shapes),
         scratch_shapes=[
-            {u: buffers(u) for u in COLUMN},
+            {u: buffers(u) for u in UNITS},
             pltpu.SMEM(touched.shape, jnp.int32),
             pltpu.SMEM(row_acc.shape, F32),
             pltpu.VMEM((SHARDS, LANES), F32),
             pltpu.VMEM((SENT_ROWS, LANES), F32),
             pltpu.SemaphoreType.DMA((SEMS,)),
-            pltpu.SemaphoreType.DMA((len(COLUMN) + 1 + 4,)),
+            pltpu.SemaphoreType.DMA((len(UNITS) + 4,)),
         ],
         compiler_params=pltpu.CompilerParams(
             collective_id=0, has_side_effects=True, vmem_limit_bytes=40 * 1024 * 1024
@@ -388,8 +380,8 @@
     )(*(
         pltpu.with_memory_space_constraint(value, pltpu.HBM)
         for value in (
-            tiles.reshape(NX, NZ, NY, NC, 8, *WHOLE),
-            tiles.reshape(NX, NZ, NY, NC, 8, 4, 2, LANES),
+            tiles.reshape(NX, NZ, NY, NC, 8, 8, LANES),
+            tiles.reshape(NX, NZ, NY, NC, 8, 2, 4, LANES),
             emb, table, row_acc, touched,
         )
     ))

time: 45.2 us -> 45.2 us (level)
  no operation moved by 1% of the time
where the time goes in v6:
time: 45.2 us; the launch traced here: 45.1 us
  Pallas kernels  44.4 us (98%)
  between operations  0.7 us (2%)
    pallas_call x1, Pallas kernels, reduce_mean(): pl.pallas_call(reduce_kernel, name='reduce_mean', out_shape=[jax.ShapeDty...  41.9 us
    pallas_call x1, Pallas kernels, body(): pl.pallas_call(update_kernel, name='update', out_shape=[jax.ShapeDtypeStr...  2.5 us

profile of v6, /device:TPU:1, one launch (start us, length us, event | category | flops | bytes accessed | tf_op | source)
XLA Modules:
  0.0 45.1 jit_solution(4211228845474290936)
XLA Ops:
  0.6 0.0 copy-start
  0.6 0.0 copy-start.1
  0.7 0.0 copy-start.2
  0.7 0.0 copy-start.3
  0.7 41.9 %reduce_mean.1 = (f32[8,1024]{1,0:T(8,128)S(1)}, f32[1,128]{1,0:T(1,128)S(1)}, f32[4096,128]{1,0:T(8,128)S(1)}, f32[512,128]{1,0:T(8,128)S(1)}, f32[512,128]{1,0...) custom-call(f32[4,8,4,2,8,8,128]{6,5,4,3,2,1,0:T(8,128)} %bitcast.10, ...), custom_call_target="tpu_custom_call" | custom-call | tf_op jit(solution)/shard_map/reduce_mean/pallas_call | solution.py:362
  42.6 0.0 copy-done
  42.6 0.0 copy-done.1
  42.6 0.0 copy-done.2
  42.6 0.0 copy-done.3
  42.6 2.5 %update.1 = (f32[8,1024]{1,0:T(8,128)}, f32[8,1024]{1,0:T(8,128)}, f32[4096,128]{1,0:T(8,128)}, f32[32,128]{1,0:T(8,128)}, f32[4096,128]{1,0:T(8,128)S(1)}) custom-call(f32[1,128]{1,0:T(1,128)S(1)} %get-tuple-element.16.norm_ref, f32[8,1024]{1,0:T(8,128)S(1)} %get-tuple-element.17.mean_ref, ...), custom_call_target="tpu_custom_call", output_to_operand_aliasing={{4}: (2, {})} | custom-call | tf_op jit(solution)/shard_map/update/pallas_call | solution.py:440
Async XLA Ops:
  0.6 41.9 %copy-start = (f32[4096]{0:T(1024)S(1)}, f32[4096]{0:T(1024)}, u32[]{:S(2)}) copy-start(f32[4096]{0:T(1024)} %row_acc_ref.1) | copy-start | bytes 49156
  0.6 41.9 %copy-start.1 = (f32[8,1024]{1,0:T(8,128)S(1)}, f32[8,1024]{1,0:T(8,128)}, u32[]{:S(2)}) copy-start(f32[8,1024]{1,0:T(8,128)} %param_ref.1) | copy-start | bytes 98308
  0.7 41.9 %copy-start.2 = (f32[8,1024]{1,0:T(8,128)S(1)}, f32[8,1024]{1,0:T(8,128)}, u32[]{:S(2)}) copy-start(f32[8,1024]{1,0:T(8,128)} %acc_ref.1) | copy-start | bytes 98308
  0.7 41.9 %copy-start.3 = (s32[512]{0:T(512)S(1)}, s32[512]{0:T(512)}, u32[]{:S(2)}) copy-start(s32[512]{0:T(512)} %touched_ref.3) | copy-start | bytes 6148
